TPU v7x, 512 devices: a whole 4x8x8 slice. The times are simulated.
512 devices in a mesh: agent: 16 (over x, z_lo, core), tp: 32 (over z_hi, y).
Axes of the slice: x: 4, y: 8, z: 8 (z_hi: 4, z_lo: 2; z = z_hi * 2 + z_lo), core: 2. Of those that a mesh axis runs over, the one named last changes fastest.
Arguments:
- tokens: bfloat16 [16, 512, 2048], P('agent', 'tp'), may hold values from -6 to 6
- targets: bfloat16 [16, 512, 2048], P('agent', 'tp'), may hold values from -6 to 6
- params: bfloat16 [16, 2048, 8192], P('agent', None, 'tp'), may hold values from -6 to 6
- tracker: bfloat16 [16, 2048, 8192], P('agent', None, 'tp'), may hold values from -6 to 6
- up_weight: bfloat16 [2048, 8192], P('agent', 'tp'), may hold values from -0.125 to 0.125
- down_weight: bfloat16 [8192, 2048], P('tp', 'agent'), may hold values from -0.0625 to 0.0625
- edge_weight: float32 [16], replicated, may hold values from 0.1 to 0.4
- step_size: float32 [1], replicated, may hold values from 0.1 to 0.5
Outputs:
- new_params: bfloat16 [16, 2048, 8192], P('agent', None, 'tp')
- new_tracker: bfloat16 [16, 2048, 8192], P('agent', None, 'tp')
All inputs are finite; a program needn't handle non-finite values.
Results may differ from a plain program's by a relative error of at most 0.033.
Values may be sent and summed in bfloat16 or wider, within the bound.
A program may use at most 64 MiB of HBM per device.

v0:
```python
import jax
import jax.numpy as jnp
from jax import lax
from jax.sharding import Mesh
from jax.sharding import PartitionSpec as P

TP = ("tp_0", "tp_1")


def passed_along(value, axis, steps):
    count = lax.axis_size(axis)
    pairs = [(source, (source + steps) % count) for source in range(count)]
    return lax.ppermute(value, axis, pairs)


def gather_turned(arrays, axis, dims):
    turned = [jnp.moveaxis(a, dim, 0) for a, dim in zip(arrays, dims)]
    widths = [t[0].size for t in turned]
    both = jnp.concatenate([t.reshape(-1, w) for t, w in zip(turned, widths)], axis=1)
    out = lax.all_gather(both, axis, axis=0, tiled=True)
    pieces = jnp.split(out, [sum(widths[:k]) for k in range(1, len(widths))], axis=1)
    return tuple(
        (
            jnp.moveaxis(b.reshape(-1, *t.shape[1:]), 0, dim)
            for b, t, dim in zip(pieces, turned, dims)
        )
    )


def side_by_side(arrays, axis, dim, along):
    widths = [a.shape[along] for a in arrays]
    both = jnp.concatenate(arrays, axis=along)
    out = lax.all_gather(both, axis, axis=dim, tiled=True)
    return tuple(jnp.split(out, [sum(widths[:k]) for k in range(1, len(widths))], axis=along))


def sum_in_order(pieces, axes, turns):
    lengths = [lax.axis_size(a) for a in axes]
    pieces = pieces.reshape(*lengths, *pieces.shape[1:])
    pieces = pieces.transpose(*turns, *range(len(axes), pieces.ndim))
    pieces = pieces.reshape(-1, *pieces.shape[len(axes) :])
    for k in turns:
        pieces = lax.psum_scatter(pieces, axes[k], scatter_dimension=0, tiled=True)
    return pieces[0]


def cut_along(array, dim, devices):
    before, after = (array.shape[:dim], array.shape[dim + 1 :])
    return jnp.moveaxis(array.reshape(*before, devices, -1, *after), dim, 0)


def sum_by_axis(array, axes, turns, dim):
    devices = lax.axis_size(axes)
    return sum_in_order(cut_along(array, dim, devices), axes, turns)


def joined_along(pieces, dim):
    lengths = list(pieces.shape[1:])
    lengths[dim] *= pieces.shape[0]
    return jnp.moveaxis(pieces, 0, dim).reshape(lengths)


def gather_in_order(array, axes, turns):
    pieces = array[None]
    for k in turns:
        pieces = lax.all_gather(pieces, axes[k], axis=0, tiled=True)
    block = [lax.axis_size(axes[k]) for k in reversed(turns)]
    pieces = pieces.reshape(*block, *array.shape)
    turned = sorted(range(len(turns)), key=lambda place: turns[len(turns) - 1 - place])
    return pieces.transpose(*turned, *range(len(turns), pieces.ndim)).reshape(-1, *array.shape)


def gather_axes(array, axes, turns, dim):
    return joined_along(gather_in_order(array, axes, turns), dim)


def on_device(tokens, targets, params, tracker, up_weight, down_weight, edge_weight, step_size):
    target_rows = targets[0]
    param = params[0]
    track = tracker[0]
    left_x, left_y = passed_along((param, track), "agent", 1)
    right_x, right_y = passed_along((param, track), "agent", -1)
    up_full, down_full = gather_turned((up_weight, down_weight), "agent", (0, 1))
    whole, whole_targets = side_by_side((tokens[0], target_rows), TP, 0, 1)
    scale = 1.0 / whole.shape[1] ** 0.5
    up = jnp.dot(whole, up_full, preferred_element_type=jnp.float32)

    def dgate_of(weights):
        gate = jnp.dot(whole, weights, preferred_element_type=jnp.float32) * scale
        sig = jax.nn.sigmoid(gate)
        hidden = (sig * gate * up).astype(jnp.bfloat16)
        partial_value = jnp.dot(hidden, down_full, preferred_element_type=jnp.float32)
        summed = sum_by_axis(partial_value.astype(jnp.bfloat16), TP, (1, 0), 0).astype(jnp.float32)
        local_err = (2.0 * (summed - target_rows.astype(jnp.float32))).astype(jnp.bfloat16)
        err = gather_axes(local_err, TP, (0, 1), 0)
        back = lax.dot_general(
            err, down_full, (((1,), (1,)), ((), ())), preferred_element_type=jnp.float32
        )
        return (back * up * sig * (1.0 + gate * (1.0 - sig))).astype(jnp.bfloat16)

    def weight_grad(dgate):
        return lax.dot_general(
            whole, dgate, (((0,), (0,)), ((), ())), preferred_element_type=jnp.float32
        )

    old_grad = weight_grad(dgate_of(param))
    count = lax.axis_size("agent")
    index = lax.axis_index("agent")
    e_right = lax.dynamic_slice_in_dim(edge_weight, index, 1)[0]
    e_left = lax.dynamic_slice_in_dim(edge_weight, (index + count - 1) % count, 1)[0]
    own = 1.0 - e_right - e_left
    track32 = track.astype(jnp.float32)
    mixed_x = (
        own * param.astype(jnp.float32)
        + e_right * right_x.astype(jnp.float32)
        + e_left * left_x.astype(jnp.float32)
    )
    mixed_y = (
        own * track32 + e_right * right_y.astype(jnp.float32) + e_left * left_y.astype(jnp.float32)
    )
    fresh = (mixed_x - step_size[0] * track32).astype(jnp.bfloat16)
    new_grad = weight_grad(dgate_of(fresh))
    fresh_track = (mixed_y + (new_grad - old_grad) * scale).astype(jnp.bfloat16)
    return (fresh[None], fresh_track[None])


def solution(mesh):
    finer = Mesh(mesh.devices.reshape(mesh.shape["agent"], 4, 8), ("agent", "tp_0", "tp_1"))
    in_specs = (
        P("agent", TP, None),
        P("agent", TP, None),
        P("agent", None, TP),
        P("agent", None, TP),
        P("agent", TP),
        P(TP, "agent"),
        P(),
        P(),
    )
    out_specs = (P("agent", None, TP), P("agent", None, TP))
    return jax.shard_map(
        on_device, mesh=finer, in_specs=in_specs, out_specs=out_specs, check_vma=False
    )
```

profile of v0, /device:TPU:1, one launch (start us, length us, event | category | flops | bytes accessed | tf_op | source)
XLA Modules:
  0.0 440.3 jit_solution(4100841673525199849)
XLA Ops:
  7.2 0.0 all-gather.5.cloned.1.call-start
  7.2 1.5 pad_maximum_fusion
  8.7 0.0 all-gather.5.cloned.1.call-update
  8.8 0.0 all-gather.7.cloned.1.call-start
  8.8 1.0 copy.21
  9.8 1.5 pad_maximum_fusion.1
  11.3 0.0 reduce-scatter.5.cloned.1.call-start
  11.4 8.7 %collective-permute-start = (bf16[2048,256]{1,0:T(8,128)(2,1)}, bf16[2048,256]{1,0:T(8,128)(2,1)S(1)}, u32[]{:S(2)}, u32[]{:S(2)}) collective-permute-start(bf16[2048,256]{1,0:T(8,128)(2,1)} %bitcast.44), channel_id=1, source_target_pairs={{0,480},{32,0},{64,32},{96,64},{128,96},{160,128},{192,160},{224,1... | collective-permute-start | bytes 3145736 | tf_op jit(solution)/shard_map/ppermute | solution.py:13
  20.1 1.9 collective-permute-start.1
  22.7 1.3 fusion.49
  25.2 13.6 %collective-permute-done = bf16[2048,256]{1,0:T(8,128)(2,1)S(1)} collective-permute-done((bf16[2048,256]{1,0:T(8,128)(2,1)}, bf16[2048,256]{1,0:T(8,128)(2,1)S(1)}, u32[]{:S(2)}, u32[]{:S(2)}) %collective-permute-start) | collective-permute-done | bytes 1048608 | tf_op jit(solution)/shard_map/ppermute | solution.py:13
  38.8 7.8 %collective-permute-done.1 = bf16[2048,256]{1,0:T(8,128)(2,1)S(1)} collective-permute-done((bf16[2048,256]{1,0:T(8,128)(2,1)}, bf16[2048,256]{1,0:T(8,128)(2,1)S(1)}, u32[]{:S(2)}, u32[]{:S(2)}) %collective-permute-start.1) | collective-permute-done | bytes 1048608 | tf_op jit(solution)/shard_map/ppermute | solution.py:13
  46.5 3.5 fusion.2
  50.0 68.5 %all-gather.5.cloned.1.call-done = bf16[512,4096]{1,0:T(8,128)(2,1)} async-done(((bf16[16,4096]{1,0:T(8,128)(2,1)}), bf16[512,4096]{1,0:T(8,128)(2,1)}) %all-gather.5.cloned.1.call-update) | async-done | bytes 4194320 | tf_op jit(solution)/shard_map/all_gather | solution.py:33
  118.6 2.3 convolution_multiply_fusion.3
  120.9 39.7 %all-gather.7.cloned.1.call-done = bf16[2048,512]{0,1:T(8,128)(2,1)} async-done(((bf16[128,512]{0,1:T(8,128)(2,1)}), bf16[2048,512]{0,1:T(8,128)(2,1)}) %all-gather.7.cloned.1.call-update) | async-done | bytes 2097168 | tf_op jit(solution)/shard_map/all_gather | solution.py:20
  160.6 2.7 fusion.15
  163.3 0.7 convolution_convert_fusion.1
  164.1 0.0 copy-done.5
  164.1 1.5 copy.22
  165.7 0.0 reduce-scatter.5.cloned.1.call-update
  165.7 0.0 reduce-scatter.9.cloned.1.call-start
  165.7 1.1 copy-done
  166.9 2.4 convolution_multiply_fusion.1
  169.3 0.7 convolution_convert_fusion
  170.0 0.0 copy-done.8
  170.1 1.5 copy.24
  171.6 0.0 reduce-scatter.7.cloned.1.call-start
  171.7 34.5 %reduce-scatter.5.cloned.1.call-done = bf16[4,16,2048]{2,1,0:T(8,128)(2,1)} async-done(((bf16[32,16,2048]{2,1,0:T(8,128)(2,1)}), bf16[4,16,2048]{2,1,0:T(8,128)(2,1)}) %reduce-scatter.5.cloned.1.call-update) | async-done | bytes 262160 | tf_op jit(solution)/shard_map/reduce_scatter | solution.py:43
  206.2 0.0 reduce-scatter.11.cloned.1.call-start
  206.2 46.8 %reduce-scatter.9.cloned.1.call-done = bf16[4,16,2048]{2,1,0:T(8,128)(2,1)} async-done(((bf16[32,16,2048]{2,1,0:T(8,128)(2,1)}), bf16[4,16,2048]{2,1,0:T(8,128)(2,1)}) %reduce-scatter.9.cloned.1.call-update) | async-done | bytes 262160 | tf_op jit(solution)/shard_map/reduce_scatter | solution.py:43
  253.1 0.0 all-gather.9.cloned.1.call-start
  253.1 33.2 %reduce-scatter.7.cloned.1.call-done = bf16[1,16,2048]{2,1,0:T(8,128)(2,1)} async-done(((bf16[4,16,2048]{2,1,0:T(8,128)(2,1)}), bf16[1,16,2048]{2,1,0:T(8,128)(2,1)}) %reduce-scatter.7.cloned.1.call-update) | async-done | bytes 65552 | tf_op jit(solution)/shard_map/reduce_scatter | solution.py:43
  286.3 29.8 %reduce-scatter.11.cloned.1.call-done = bf16[1,16,2048]{2,1,0:T(8,128)(2,1)} async-done(((bf16[4,16,2048]{2,1,0:T(8,128)(2,1)}), bf16[1,16,2048]{2,1,0:T(8,128)(2,1)}) %reduce-scatter.11.cloned.1.call-update) | async-done | bytes 65552 | tf_op jit(solution)/shard_map/reduce_scatter | solution.py:43
  316.1 0.9 fusion.43
  317.0 11.9 %all_gather.20 = bf16[4,16,2048]{2,1,0:T(8,128)(2,1)} all-gather(bf16[1,16,2048]{2,1,0:T(8,128)(2,1)S(1)} %get-tuple-element.3), channel_id=1, replica_groups=mesh['agent'=16,'tp_0'=4,'tp_1'=8] {'tp_0'}, dimensions={0}, use_global_device_ids=true | all-gather | bytes 327680 | tf_op jit(solution)/shard_map/all_gather | solution.py:66
  328.9 0.0 all-gather.9.cloned.1.call-update
  328.9 0.0 all-gather.11.cloned.1.call-start
  329.0 13.8 %all_gather.22 = bf16[4,16,2048]{2,1,0:T(8,128)(2,1)} all-gather(bf16[1,16,2048]{2,1,0:T(8,128)(2,1)S(1)} %get-tuple-element.2), channel_id=1, replica_groups=mesh['agent'=16,'tp_0'=4,'tp_1'=8] {'tp_0'}, dimensions={0}, use_global_device_ids=true | all-gather | bytes 327680 | tf_op jit(solution)/shard_map/all_gather | solution.py:66
  342.8 0.0 all-gather.11.cloned.1.call-update
  342.8 10.4 %collective-permute-start.2 = (bf16[2048,256]{1,0:T(8,128)(2,1)S(1)}, bf16[2048,256]{1,0:T(8,128)(2,1)}, u32[]{:S(2)}, u32[]{:S(2)}) collective-permute-start(bf16[2048,256]{1,0:T(8,128)(2,1)S(1)} %bitcast.46), channel_id=1, source_target_pairs={{0,480},{32,0},{64,32},{96,64},{128,96},{160,128},{192,160},{224,1... | collective-permute-start | bytes 3145736 | tf_op jit(solution)/shard_map/ppermute | solution.py:13
  353.3 1.9 collective-permute-start.3
  355.2 17.5 %all-gather.9.cloned.1.call-done = bf16[32,16,2048]{2,1,0:T(8,128)(2,1)} async-done(((bf16[4,16,2048]{2,1,0:T(8,128)(2,1)}), bf16[32,16,2048]{2,1,0:T(8,128)(2,1)}) %all-gather.9.cloned.1.call-update) | async-done | bytes 2097168 | tf_op jit(solution)/shard_map/all_gather | solution.py:66
  372.7 3.2 copy.23
  375.9 41.1 %all-gather.11.cloned.1.call-done = bf16[32,16,2048]{2,1,0:T(8,128)(2,1)} async-done(((bf16[4,16,2048]{2,1,0:T(8,128)(2,1)}), bf16[32,16,2048]{2,1,0:T(8,128)(2,1)}) %all-gather.11.cloned.1.call-update) | async-done | bytes 2097168 | tf_op jit(solution)/shard_map/all_gather | solution.py:66
  416.9 1.7 copy.25
  418.7 6.6 %fusion.13 = f32[2048,256]{1,0:T(8,128)} fusion(bf16[512,4096]{1,0:T(8,128)(2,1)} %all-gather.5.cloned.1.call-done, f32[512,256]{1,0:T(8,128)} %copy-done.7, f32[512,256]{1,0:T(8,128)} %copy-done.5, bf16[512,2048]{1,0:T(8,128)(2,1)} %bitcast.41, bf16[2048,512]{0,1:T(8,128)(2,1)} %all-gather.7.cloned.1.call-done), kind=kOutput, calls=%fused_computation.22 | convolution fusion | flops 1075052544 | bytes 8388608 | tf_op jit(solution)/shard_map/dot_general | solution.py:102
  425.2 8.2 %fusion.20 = bf16[1,2048,256]{2,1,0:T(8,128)(2,1)} fusion(f32[2048,256]{1,0:T(8,128)} %fusion.13, bf16[512,4096]{1,0:T(8,128)(2,1)} %all-gather.5.cloned.1.call-done, bf16[2048,256]{1,0:T(8,128)(2,1)} %collective-permute-done.3, bf16[2048,256]{1,0:T(8,128)(2,1)} %collective-permute-done.2, f32[]{:T(128)} %bitcast.1, f32[]{:T(128)} %bitcast, f32[]{:T(128)S(6)} %sub.31, ...), kind=kOutput, calls=%fused_computation.27 | convolution fusion | flops 1081344000 | bytes 12583940 | tf_op jit(solution)/shard_map/dot_general | solution.py:102
  (21 shorter events, 0.1 us)
Async XLA Ops:
  7.2 111.4 %all-gather.5.cloned.1.call-start = ((), (), s32[]{:S(2)}) async-start(), calls=%async_computation.4 | async-start | bytes 4325376 | tf_op jit(solution)/shard_map/all_gather | solution.py:33
  8.8 151.8 %all-gather.7.cloned.1.call-start = ((), (), s32[]{:S(2)}) async-start(), calls=%async_computation.5 | async-start | bytes 2228224 | tf_op jit(solution)/shard_map/all_gather | solution.py:20
  11.3 194.9 %reduce-scatter.5.cloned.1.call-start = ((), (), s32[]{:S(2)}) async-start(), calls=%async_computation.6 | async-start | bytes 2359296 | tf_op jit(solution)/shard_map/reduce_scatter | solution.py:43
  11.4 27.4 %collective-permute-start = (bf16[2048,256]{1,0:T(8,128)(2,1)}, bf16[2048,256]{1,0:T(8,128)(2,1)S(1)}, u32[]{:S(2)}, u32[]{:S(2)}) collective-permute-start(bf16[2048,256]{1,0:T(8,128)(2,1)} %bitcast.44), channel_id=1, source_target_pairs={{0,480},{32,0},{64,32},{96,64},{128,96},{160,128},{192,160},{224,1... | collective-permute-start | bytes 3145736 | tf_op jit(solution)/shard_map/ppermute | solution.py:13
  20.1 26.4 %collective-permute-start.1 = (bf16[2048,256]{1,0:T(8,128)(2,1)}, bf16[2048,256]{1,0:T(8,128)(2,1)S(1)}, u32[]{:S(2)}, u32[]{:S(2)}) collective-permute-start(bf16[2048,256]{1,0:T(8,128)(2,1)} %bitcast.45), channel_id=1, source_target_pairs={{0,32},{32,64},{64,96},{96,128},{128,160},{160,192},{192,224},{224... | collective-permute-start | bytes 3145736 | tf_op jit(solution)/shard_map/ppermute | solution.py:13
  50.0 70.9 %copy-start.2 = (bf16[2048,256]{1,0:T(8,128)(2,1)}, bf16[2048,256]{1,0:T(8,128)(2,1)S(1)}, u32[]{:S(2)}) copy-start(bf16[2048,256]{1,0:T(8,128)(2,1)S(1)} %fusion.2) | copy-start | bytes 3145732
  120.9 42.4 %copy-start.7 = (f32[512,256]{1,0:T(8,128)}, f32[512,256]{1,0:T(8,128)S(1)}, u32[]{:S(2)}) copy-start(f32[512,256]{1,0:T(8,128)S(1)} %convolution_multiply_fusion.3) | copy-start | bytes 1572868
  160.6 2.8 copy-start.4
  163.3 0.8 copy-start.5
  165.7 1.2 copy-start
  165.7 87.4 %reduce-scatter.9.cloned.1.call-start = ((), (), s32[]{:S(2)}) async-start(), calls=%async_computation.9 | async-start | bytes 2359296 | tf_op jit(solution)/shard_map/reduce_scatter | solution.py:43
  166.9 2.4 copy-start.6
  169.3 0.8 copy-start.8
  171.6 144.5 %copy-start.3 = (bf16[1,16,2048]{2,1,0:T(8,128)(2,1)S(1)}, bf16[1,16,2048]{2,1,0:T(8,128)(2,1)}, u32[]{:S(2)}) copy-start(bf16[1,16,2048]{2,1,0:T(8,128)(2,1)} %param.9) | copy-start | bytes 196612
  171.6 171.2 %copy-start.1 = (bf16[1,2048,256]{2,1,0:T(8,128)(2,1)S(1)}, bf16[1,2048,256]{2,1,0:T(8,128)(2,1)}, u32[]{:S(2)}) copy-start(bf16[1,2048,256]{2,1,0:T(8,128)(2,1)} %param.11) | copy-start | bytes 3145732
  171.6 114.7 %reduce-scatter.7.cloned.1.call-start = ((), (), s32[]{:S(2)}) async-start(), calls=%async_computation.7 | async-start | bytes 327680 | tf_op jit(solution)/shard_map/reduce_scatter | solution.py:43
  206.2 109.9 %reduce-scatter.11.cloned.1.call-start = ((), (), s32[]{:S(2)}) async-start(), calls=%async_computation.10 | async-start | bytes 327680 | tf_op jit(solution)/shard_map/reduce_scatter | solution.py:43
  253.1 119.6 %all-gather.9.cloned.1.call-start = ((), (), s32[]{:S(2)}) async-start(), calls=%async_computation.8 | async-start | bytes 2359296 | tf_op jit(solution)/shard_map/all_gather | solution.py:66
  328.9 88.0 %all-gather.11.cloned.1.call-start = ((), (), s32[]{:S(2)}) async-start(), calls=%async_computation.11 | async-start | bytes 2359296 | tf_op jit(solution)/shard_map/all_gather | solution.py:66
  342.8 82.4 %collective-permute-start.2 = (bf16[2048,256]{1,0:T(8,128)(2,1)S(1)}, bf16[2048,256]{1,0:T(8,128)(2,1)}, u32[]{:S(2)}, u32[]{:S(2)}) collective-permute-start(bf16[2048,256]{1,0:T(8,128)(2,1)S(1)} %bitcast.46), channel_id=1, source_target_pairs={{0,480},{32,0},{64,32},{96,64},{128,96},{160,128},{192,160},{224,1... | collective-permute-start | bytes 3145736 | tf_op jit(solution)/shard_map/ppermute | solution.py:13
  353.3 72.0 %collective-permute-start.3 = (bf16[2048,256]{1,0:T(8,128)(2,1)S(1)}, bf16[2048,256]{1,0:T(8,128)(2,1)}, u32[]{:S(2)}, u32[]{:S(2)}) collective-permute-start(bf16[2048,256]{1,0:T(8,128)(2,1)S(1)} %bitcast.47), channel_id=1, source_target_pairs={{0,32},{32,64},{64,96},{96,128},{128,160},{160,192},{192,224},{224... | collective-permute-start | bytes 3145736 | tf_op jit(solution)/shard_map/ppermute | solution.py:13
Sparse Core Ops, SparseCore 0:
  11.7 106.7 all-gather.4
  120.6 39.9 all-gather.6
  165.8 40.2 reduce-scatter.4
  208.9 44.1 reduce-scatter.8
  255.7 30.5 reduce-scatter.6
  288.9 27.0 reduce-scatter.10
  329.1 43.6 all-gather.8
  374.8 42.1 all-gather.10
where the time goes:
time: 444 us; the launch traced here: 440 us
  waiting for transfers between devices  332 us (75%)
  blocking collectives  25.7 us (6%)
  matrix products  23.7 us (5%)
  starting transfers between devices  23.3 us (5%)
  between operations  16.1 us (4%)
  local copies, waits for them, and re-layouts  11.5 us (3%)
  other arithmetic  7.45 us (2%)
    reduce_scatter x4, waiting for transfers between devices, sum_in_order(): pieces = lax.psum_scatter(pieces, axes[k], scatter_dimension=0, tiled=True)  144 us
    all_gather x1, waiting for transfers between devices, side_by_side(): out = lax.all_gather(both, axis, axis=dim, tiled=True)  68.5 us
    all_gather x2, waiting for transfers between devices, gather_in_order(): pieces = lax.all_gather(pieces, axes[k], axis=0, tiled=True)  58.6 us
    all_gather x1, waiting for transfers between devices, gather_turned(): out = lax.all_gather(both, axis, axis=0, tiled=True)  39.7 us
    all_gather x2, blocking collectives, gather_in_order(): pieces = lax.all_gather(pieces, axes[k], axis=0, tiled=True)  25.7 us
    ppermute x4, starting transfers between devices, passed_along(): return lax.ppermute(value, axis, pairs)  23 us
    ppermute x4, waiting for transfers between devices, passed_along(): return lax.ppermute(value, axis, pairs)  21.3 us
    dot_general x2, matrix products, weight_grad(): lax.dot_general(whole, dgate, (((0,), (0,)), ((), ())), preferred_element...  14.8 us
  transfers between devices with their start and end apart: 12, of which 10 were waited for; matrix products, arithmetic and copies ran while one was open for 6% of the time, Pallas kernels for 0%

commit v1 on v0

v1 whole, which is shorter than its diff:
```python
import functools

import jax
import jax.numpy as jnp
from jax import lax
from jax.experimental import pallas as pl
from jax.experimental.pallas import tpu as pltpu
from jax.sharding import PartitionSpec as P

MESH = pl.DeviceIdType.MESH
BF16 = jnp.bfloat16
F32 = jnp.float32
ORDER = (0, 7, 1, 6, 2, 5, 3, 4)
TRACK_PIECES = 4


class Plan:
    def __init__(self):
        self.count = 0

    def take(self, *shape):
        size = 1
        for n in shape:
            size *= n
        base = self.count
        self.count += size

        def number(*index):
            flat = 0
            for i, n in zip(index, shape):
                flat = flat * n + i
            return base + flat

        return number


plan = Plan()
TZ = plan.take(4)
TY = plan.take(2, 5, 4)
UZ, UX, UF, UC = plan.take(1), plan.take(2), plan.take(2), plan.take(1)
DZ, DY = plan.take(1), plan.take(2, 5)
DX, DF, DC = plan.take(2, 8), plan.take(2, 8), plan.take(8)
PI, PO, TI, TO = plan.take(1), plan.take(1), plan.take(1), plan.take(TRACK_PIECES)
HI, RS, EG, BK = plan.take(2, 8), plan.take(2, 4), plan.take(2, 4), plan.take(2, 8)
SEMS = plan.count


def kernel(
    edge, step, tokens, targets, params, tracker, up_w, down_w, fresh_out, track_out,
    tok, tgt, pbuf, tbuf, pin, pof, tin, tof, fresh, upb, dwn, upv, fac, hsend, hall,
    psend, prec, eall, bsend, brec, dd, trk, ssem, rsem, lsem,
):
    a = lax.axis_index("agent")
    t = lax.axis_index("tp")
    x, zl, c = a // 4, (a // 2) % 2, a % 2
    zh, y = t // 8, t % 8
    scale = 2048.0 ** -0.5

    def along_y(r):
        return (a, zh * 8 + (y + r) % 8)

    def along_z(q):
        return (a, ((zh + q) % 4) * 8 + y)

    def along_x(r):
        return ((a + 4 * r + 16) % 16, t)

    other_core = (a + 1 - 2 * c, t)
    off_chip = ((a + 2 * c + 15) % 16, t)
    other_z = (a + 2 - 4 * zl, t)

    def cols(first, n):
        return pl.ds(first, n)

    local = []

    def fetch(src, dst):
        copy = pltpu.make_async_copy(src, dst, lsem.at[len(local)])
        copy.start()
        local.append(copy)
        return copy

    up_own = upb.at[x, zl, c]
    got_tok = fetch(tokens.at[0], tok.at[cols(0, 16)])
    got_up = fetch(up_w, up_own)
    got_down = fetch(down_w, dwn.at[cols(0, 256), cols(0, 128)])
    got_p = fetch(params.at[0], pbuf)
    got_t = fetch(tracker.at[0], tbuf)
    got_tgt = []
    for rc in range(2):
        for rx in range(4):
            for rz in range(2):
                who = ((x + rx) % 4) * 4 + ((zl + rz) % 2) * 2 + (c + rc) % 2
                src = targets.at[0, :, pl.ds(pl.multiple_of(who * 128, 128), 128)]
                got_tgt.append(fetch(src, tgt.at[:, cols(rc * 1024 + rx * 256 + rz * 128, 128)]))

    barrier = pltpu.get_barrier_semaphore()
    peers = [other_core, off_chip, other_z, along_x(1), along_x(-1)]
    peers += [along_y(r) for r in range(1, 8)] + [along_z(q) for q in range(1, 4)]
    for peer in peers:
        pl.semaphore_signal(barrier, inc=1, device_id=peer, device_id_type=MESH)
    pl.semaphore_wait(barrier, len(peers))

    sent = []

    def message(src, dst, peer, k):
        return pltpu.make_async_remote_copy(
            src_ref=src, dst_ref=dst, send_sem=ssem.at[k], recv_sem=rsem.at[k],
            device_id=peer, device_id_type=MESH,
        )

    def send(src, dst, peer, k):
        copy = message(src, dst, peer, k)
        copy.start()
        sent.append(copy)

    def arrive(dst, k):
        message(dst, dst, other_core, k).wait_recv()

    def tok_at(r, q):
        return tok.at[cols((r % 8) * 64 + (q % 4) * 16, 16)]

    def dwn_at(r, rx, first=0, rows=256):
        return dwn.at[cols((r % 8) * 256 + first, rows), cols(rx * 256, 256)]

    def tok_steps(way, q):
        return 4 if (q < 2) == (way == 0) else 3

    def tok_step(way, s, q):
        sign = 1 if way == 0 else -1
        send(tok_at(-sign * (s - 1), q), tok_at(-sign * s, q), along_y(sign), TY(way, s, q))

    def tok_wait(way, s, q):
        sign = 1 if way == 0 else -1
        arrive(tok_at(-sign * s, q), TY(way, s, q))

    def dwn_half(way, s):
        return (0, 256) if s < 4 else (128 * way, 128)

    def dwn_step(way, s):
        sign = 1 if way == 0 else -1
        half = dwn_half(way, s)
        send(
            dwn_at(-sign * (s - 1), 0, *half), dwn_at(-sign * s, 0, *half),
            along_y(sign), DY(way, s),
        )

    def dwn_wait(way, s):
        sign = 1 if way == 0 else -1
        arrive(dwn_at(-sign * s, 0, *dwn_half(way, s)), DY(way, s))

    def x_first(r):
        send(dwn_at(r, 0), dwn_at(r, 3), along_x(1), DX(0, r))
        send(dwn_at(r, 0), dwn_at(r, 1), along_x(-1), DX(1, r))

    def x_second(r):
        arrive(dwn_at(r, 3), DX(0, r))
        send(dwn_at(r, 3, 0, 128), dwn_at(r, 2, 0, 128), along_x(1), DF(0, r))
        arrive(dwn_at(r, 1), DX(1, r))
        send(dwn_at(r, 1, 128, 128), dwn_at(r, 2, 128, 128), along_x(-1), DF(1, r))

    def core_half(r, rc):
        return dwn.at[cols((r % 8) * 256, 256), cols(rc * 1024, 1024)]

    def x_third(r):
        arrive(dwn_at(r, 2, 0, 128), DF(0, r))
        arrive(dwn_at(r, 2, 128, 128), DF(1, r))
        send(core_half(r, 0), core_half(r, 1), other_core, DC(r))

    got_tok.wait()
    for d in (1, 3, 2):
        send(tok_at(0, 0), tok_at(0, -d), along_z(d), TZ(d))
    for way in range(2):
        tok_step(way, 1, 0)
    got_up.wait()
    send(up_own, up_own, other_z, UZ(0))
    got_down.wait()
    send(
        dwn.at[cols(0, 256), cols(0, 128)], dwn.at[cols(0, 256), cols(128, 128)], other_z, DZ(0)
    )
    got_p.wait()
    send(pbuf, pof, off_chip, PO(0))
    send(pbuf, pin, other_core, PI(0))
    got_t.wait()
    send(tbuf, tin, other_core, TI(0))
    for copy in got_tgt:
        copy.wait()

    for d in (1, 3, 2):
        arrive(tok_at(0, -d), TZ(d))
        for way in range(2):
            tok_step(way, 1, 4 - d)
    arrive(upb.at[x, 1 - zl, c], UZ(0))
    send(upb.at[x, :, c], upb.at[x, :, c], along_x(1), UX(0))
    send(upb.at[x, :, c], upb.at[x, :, c], along_x(-1), UX(1))
    arrive(dwn.at[cols(0, 256), cols(128, 128)], DZ(0))
    dwn_step(0, 1)
    dwn_step(1, 1)
    x_first(0)

    for s in range(1, 5):
        for q in (0, 3, 1, 2):
            for way in range(2):
                if s <= tok_steps(way, q):
                    tok_wait(way, s, q)
                    if s < tok_steps(way, q):
                        tok_step(way, s + 1, q)
        for way in range(2):
            dwn_wait(way, s)
            if s < 4:
                dwn_step(way, s + 1)
        for r in (8 - s, s)[: 2 if s < 4 else 1]:
            x_first(r)
        if s == 1:
            below, above = (x + 3) % 4, (x + 1) % 4
            arrive(upb.at[below, :, c], UX(0))
            send(upb.at[below, 0, c], upb.at[below, 0, c], along_x(1), UF(0))
            arrive(upb.at[above, :, c], UX(1))
            send(upb.at[above, 1, c], upb.at[above, 1, c], along_x(-1), UF(1))
            x_second(0)
        if s == 2:
            across = (x + 2) % 4
            arrive(upb.at[across, 0, c], UF(0))
            arrive(upb.at[across, 1, c], UF(1))
            send(upb.at[:, :, c], upb.at[:, :, c], other_core, UC(0))
            x_third(0)
            x_second(7)
            x_second(1)
        if s == 3:
            x_third(7)
            x_third(1)
            x_second(6)
            x_second(2)
        if s == 4:
            x_second(5)
            x_second(3)
            x_third(6)
            x_third(2)

    def rows256(i):
        return pl.ds(pl.multiple_of(i * 256, 256), 256)

    arrive(upb.at[:, :, 1 - c], UC(0))

    @pl.loop(0, 2)
    def _(i):
        rows = rows256(i)
        total = jnp.zeros((256, 256), F32)
        for k in range(8):
            total += jnp.dot(
                tok[rows, k * 256 : (k + 1) * 256],
                upb[k // 2, k % 2].reshape(256, 256),
                preferred_element_type=F32,
            )
        upv[rows, :] = total

    def hidden_of(p, weights):
        @pl.loop(0, 2)
        def _(i):
            rows = rows256(i)
            gate = jnp.dot(tok[rows, :], weights[...], preferred_element_type=F32) * scale
            sig = jax.nn.sigmoid(gate)
            up = upv[rows, :]
            hsend[p, rows, :] = (sig * gate * up).astype(BF16)
            fac[p, rows, :] = up * sig * (1.0 + gate * (1.0 - sig))

        for r in (1, 7, 2, 6, 3, 5, 4):
            send(
                hsend.at[p, cols(r * 64, 64)], hall.at[p, :, cols((8 - r) * 256, 256)],
                along_y(r), HI(p, r),
            )
        hall[p, :, 0:256] = hsend[p, 0:64, :]

    hidden_of(0, pbuf)
    x_second(4)

    e_off = edge[(a + c + 15) % 16]
    e_in = edge[(a + 16 - c) % 16]
    own = 1.0 - e_off - e_in
    eta = step[0]
    arrive(pin, PI(0))
    arrive(pof, PO(0))

    def track_piece(k):
        return tof.at[cols(k * (2048 // TRACK_PIECES), 2048 // TRACK_PIECES)]

    def track_send(k):
        rows = cols(k * (2048 // TRACK_PIECES), 2048 // TRACK_PIECES)
        send(tbuf.at[rows], tof.at[rows], off_chip, TO(k))

    track_send(0)
    track_send(1)

    @pl.loop(0, 8)
    def _(i):
        rows = rows256(i)
        mixed = own * pbuf[rows, :].astype(F32)
        mixed += e_off * pof[rows, :].astype(F32) + e_in * pin[rows, :].astype(F32)
        fresh[rows, :] = (mixed - eta * tbuf[rows, :].astype(F32)).astype(BF16)

    fresh_copy = pltpu.make_async_copy(fresh, fresh_out.at[0], lsem.at[len(local)])
    fresh_copy.start()
    hidden_of(1, fresh)
    x_third(5)
    x_third(3)
    x_third(4)
    for r in ORDER:
        arrive(core_half(r, 1), DC(r))

    def partial_of(p):
        for r in range(1, 8):
            arrive(hall.at[p, :, cols((8 - r) * 256, 256)], HI(p, r))

        @pl.loop(0, 8)
        def _(i):
            part = jnp.dot(hall[p], dwn[:, rows256(i)], preferred_element_type=F32)
            psend[p, :, rows256(i)] = part.astype(BF16)

        for q in (1, 3, 2):
            send(psend.at[p, cols(q * 16, 16)], prec.at[p, 4 - q], along_z(q), RS(p, q))

    partial_of(0)
    partial_of(1)

    def err_of(p):
        total = psend[p, 0:16, :].astype(F32)
        for q in (1, 3, 2):
            arrive(prec.at[p, 4 - q], RS(p, q))
            total += prec[p, 4 - q].astype(F32)
        eall[p, 0:16, :] = (2.0 * (total - tgt[...].astype(F32))).astype(BF16)
        for q in (1, 3, 2):
            send(
                eall.at[p, cols(0, 16)], eall.at[p, cols((4 - q) * 16, 16)], along_z(q), EG(p, q)
            )

    err_of(0)
    err_of(1)
    for k in range(2, TRACK_PIECES):
        track_send(k)

    def back_block(p, r):
        return lax.dot_general(
            eall[p], dwn[pl.ds(pl.multiple_of(r * 256, 256), 256), :],
            (((1,), (1,)), ((), ())), preferred_element_type=F32,
        ).astype(BF16)

    def back_message(p, r):
        rows = pl.ds(pl.multiple_of(r * 64, 64), 64)
        land = pl.ds(pl.multiple_of((8 - r) * 64, 64), 64)
        return message(bsend.at[p, rows], brec.at[p, land], along_y(r), BK(p, 0) + r)

    def back_of(p):
        for q in (1, 3, 2):
            arrive(eall.at[p, cols((4 - q) * 16, 16)], EG(p, q))

        @pl.loop(1, 8)
        def _(r):
            bsend[p, pl.ds(pl.multiple_of(r * 64, 64), 64), :] = back_block(p, r)
            back_message(p, r).start()

        brec[p, 0:64, :] = back_block(p, 0)

    back_of(0)
    back_of(1)
    for p in range(2):

        @pl.loop(1, 8)
        def _(r):
            land = pl.ds(pl.multiple_of((8 - r) * 64, 64), 64)
            message(brec.at[p, land], brec.at[p, land], other_core, BK(p, 0) + r).wait_recv()

    dd[...] = (
        brec[1].astype(F32) * fac[1] - brec[0].astype(F32) * fac[0]
    ).astype(BF16)
    arrive(tin, TI(0))
    for k in range(TRACK_PIECES):
        arrive(track_piece(k), TO(k))

    @pl.loop(0, 8)
    def _(i):
        rows = rows256(i)
        change = lax.dot_general(
            tok[:, rows], dd[...], (((0,), (0,)), ((), ())), preferred_element_type=F32
        )
        mixed = own * tbuf[rows, :].astype(F32)
        mixed += e_off * tof[rows, :].astype(F32) + e_in * tin[rows, :].astype(F32)
        trk[rows, :] = (mixed + change * scale).astype(BF16)

    track_copy = pltpu.make_async_copy(trk, track_out.at[0], lsem.at[len(local) + 1])
    track_copy.start()
    for copy in sent:
        copy.wait_send()
    for p in range(2):

        @pl.loop(1, 8)
        def _(r):
            back_message(p, r).wait_send()

    fresh_copy.wait()
    track_copy.wait()


def on_device(tokens, targets, params, tracker, up_weight, down_weight, edge_weight, step_size):
    hbm = pl.BlockSpec(memory_space=pltpu.HBM)
    smem = pl.BlockSpec(memory_space=pltpu.SMEM)
    block = pltpu.VMEM((2048, 256), BF16)
    out = jax.ShapeDtypeStruct(params.shape, BF16)
    return pl.pallas_call(
        kernel,
        out_shape=(out, out),
        in_specs=[smem, smem] + [hbm] * 6,
        out_specs=(hbm, hbm),
        scratch_shapes=[
            pltpu.VMEM((512, 2048), BF16),
            pltpu.VMEM((16, 2048), BF16),
            block, block, block, block, block, block, block,
            pltpu.VMEM((4, 2, 2, 128, 256), BF16),
            pltpu.VMEM((2048, 2048), BF16),
            pltpu.VMEM((512, 256), F32),
            pltpu.VMEM((2, 512, 256), F32),
            pltpu.VMEM((2, 512, 256), BF16),
            pltpu.VMEM((2, 64, 2048), BF16),
            pltpu.VMEM((2, 64, 2048), BF16),
            pltpu.VMEM((2, 4, 16, 2048), BF16),
            pltpu.VMEM((2, 64, 2048), BF16),
            pltpu.VMEM((2, 512, 256), BF16),
            pltpu.VMEM((2, 512, 256), BF16),
            pltpu.VMEM((512, 256), BF16),
            block,
            pltpu.SemaphoreType.DMA((SEMS,)),
            pltpu.SemaphoreType.DMA((SEMS,)),
            pltpu.SemaphoreType.DMA((24,)),
        ],
        compiler_params=pltpu.CompilerParams(
            collective_id=0, has_side_effects=True, vmem_limit_bytes=56 * 1024 * 1024
        ),
    )(edge_weight, step_size, tokens, targets, params, tracker, up_weight, down_weight)


def solution(mesh):
    in_specs = (
        P("agent", "tp", None),
        P("agent", "tp", None),
        P("agent", None, "tp"),
        P("agent", None, "tp"),
        P("agent", "tp"),
        P("tp", "agent"),
        P(),
        P(),
    )
    out_specs = (P("agent", None, "tp"), P("agent", None, "tp"))
    return jax.shard_map(
        on_device, mesh=mesh, in_specs=in_specs, out_specs=out_specs, check_vma=False
    )
```

time: 444 us -> 132 us (0.30)
  waiting for transfers between devices: 332 us -> 0 us
  Pallas kernels: 0 us -> 127 us
  blocking collectives: 25.7 us -> 0 us
  matrix products: 23.7 us -> 0 us
  starting transfers between devices: 23.3 us -> 0 us
  between operations: 16.1 us -> 1.3 us
  local copies, waits for them, and re-layouts: 11.5 us -> 3.32 us
  other arithmetic: 7.45 us -> 0 us
    all_gather x4 -> x0, waiting for transfers between devices: 167 us -> none  [the longest x1 68.5 us: side_by_side(): out = lax.all_gather(both, axis, axis=dim, tiled=True)]
    reduce_scatter x4 -> x0, waiting for transfers between devices: 144 us -> none  [sum_in_order(): pieces = lax.psum_scatter(pieces, axes[k], scatter_dimension=0, tiled=True)]
    pallas_call x0 -> x1, Pallas kernels: none -> 127 us  [on_device(): pl.pallas_call(kernel, out_shape=(out, out), in_specs=[smem, smem] + [hbm...]
    all_gather x2 -> x0, blocking collectives: 25.7 us -> none  [gather_in_order(): pieces = lax.all_gather(pieces, axes[k], axis=0, tiled=True)]
    dot_general x7 -> x0, matrix products: 23.7 us -> none  [the longest x2 14.8 us: weight_grad(): lax.dot_general(whole, dgate, (((0,), (0,)), ((), ())), preferred_element...]
    ppermute x4 -> x0, starting transfers between devices: 23 us -> none  [passed_along(): return lax.ppermute(value, axis, pairs)]
    ppermute x4 -> x0, waiting for transfers between devices: 21.3 us -> none  [passed_along(): return lax.ppermute(value, axis, pairs)]
    transpose x4 -> x0, local copies, waits for them, and re-layouts: 7.95 us -> none  [the longest x2 4.9 us: gather_in_order(): pieces.transpose(*turned, *range(len(turns), pieces.ndim))]
  transfers between devices with their start and end apart: 12 -> 0, of which waited for: 10 -> 0; matrix products, arithmetic and copies ran while one was open for 6% -> 0% of each run, Pallas kernels for 0% -> 0%
where the time goes in v1:
time: 132 us; the launch traced here: 131 us
  Pallas kernels  127 us (96%)
  local copies, waits for them, and re-layouts  3.32 us (3%)
    pallas_call x1, Pallas kernels, on_device(): pl.pallas_call(kernel, out_shape=(out, out), in_specs=[smem, smem] + [hbm...  127 us
    unnamed x4, local copies, waits for them, and re-layouts  3.32 us

profile of v1, /device:TPU:1, one launch (start us, length us, event | category | flops | bytes accessed | tf_op | source)
XLA Modules:
  0.0 131.3 jit_solution(5934892045158767526)
XLA Ops:
  1.3 126.7 %shard_map.95 = (bf16[1,2048,256]{2,1,0:T(8,128)(2,1)}, bf16[1,2048,256]{2,1,0:T(8,128)(2,1)}) custom-call(f32[16]{0:T(128)} %edge.1, f32[1]{0:T(128)S(6)} %copy.12.step, bf16[1,16,2048]{2,1,0:T(8,128)(2,1)} %tokens.1, bf16[1,16,2048]{2,1,0:T(8,128)(2,1)} %targets.1, bf16[1,2048,256]{2,1,0:T(8,128)(2,1)} %params.1, bf16[1,2048,256]{2,1,0:T(8,128)(2,1)} %tracker.1, ...), custom_call_target="tpu_custom_call" | custom-call | tf_op jit(solution)/shard_map/pallas_call | solution.py:408
  128.0 0.0 copy-start
  128.0 2.4 %copy.13 = bf16[1,2048,256]{2,1,0:T(8,128)(2,1)} copy(bf16[1,2048,256]{2,1,0:T(8,128)(2,1)} %get-tuple-element.4) | data formatting | bytes 2097152
  130.3 0.0 copy-done
  130.3 1.0 copy.14
Async XLA Ops:
  128.0 2.4 %copy-start = (bf16[1,2048,256]{2,1,0:T(8,128)(2,1)S(1)}, bf16[1,2048,256]{2,1,0:T(8,128)(2,1)}, u32[]{:S(2)}) copy-start(bf16[1,2048,256]{2,1,0:T(8,128)(2,1)} %get-tuple-element.5) | copy-start | bytes 3145732

commit v2 on v1

v2 whole, which is shorter than its diff:
```python
import functools

import jax
import jax.numpy as jnp
from jax import lax
from jax.experimental import pallas as pl
from jax.experimental.pallas import tpu as pltpu
from jax.sharding import PartitionSpec as P

MESH = pl.DeviceIdType.MESH
BF16 = jnp.bfloat16
F32 = jnp.float32
ORDER = (0, 7, 1, 6, 2, 5, 3, 4)
NEAR = 224
FAR_FIRST = (4, 3, 5, 2, 6, 1, 7)


class Plan:
    def __init__(self):
        self.count = 0

    def take(self, *shape):
        size = 1
        for n in shape:
            size *= n
        base = self.count
        self.count += size

        def number(*index):
            flat = 0
            for i, n in zip(index, shape):
                flat = flat * n + i
            return base + flat

        return number


plan = Plan()
TZ = plan.take(2, 2)
TY = plan.take(2, 5, 4)
UZ, UX, UF, UC = plan.take(1), plan.take(2), plan.take(2), plan.take(1)
DZ, DY, EY = plan.take(1), plan.take(2, 5), plan.take(2, 5)
DX, DF, DC = plan.take(2, 8), plan.take(2, 8), plan.take(8)
D0, DB = plan.take(2), plan.take(2)
PI, PO, TI, TO = plan.take(1), plan.take(3), plan.take(1), plan.take(2)
PR, TR = plan.take(1), plan.take(1)
HI, BK = plan.take(2, 8), plan.take(2, 8)
RS, EG = plan.take(2, 3, 2), plan.take(2, 2, 2)
SEMS = plan.count


def kernel(
    edge, step, tokens, targets, params, tracker, up_w, down_w, fresh_out, track_out,
    tok, tgt, pbuf, tbuf, pin, pof, tin, tof, fresh, upb, dwn, upv, fac, hsend, hall,
    psend, pmid, prec, eall, bsend, brec, dd, trk, prel, trel, turned, mixed_y, ssem, rsem, lsem,
):
    a = lax.axis_index("agent")
    t = lax.axis_index("tp")
    x, zl, c = a // 4, (a // 2) % 2, a % 2
    zh, y = t // 8, t % 8
    scale = 2048.0 ** -0.5

    def along_y(r):
        return (a, zh * 8 + (y + r + 8) % 8)

    def along_z(q):
        return (a, ((zh + q + 4) % 4) * 8 + y)

    def along_x(r):
        return ((a + 4 * r + 16) % 16, t)

    other_core = (a + 1 - 2 * c, t)
    off_chip = ((a + 2 * c + 15) % 16, t)
    other_z = (a + 2 - 4 * zl, t)
    beyond = ((a + 6 * c + 13) % 16, t)
    diagonal = c == zl

    def cols(first, n):
        return pl.ds(first, n)

    local = []

    def fetch(src, dst):
        copy = pltpu.make_async_copy(src, dst, lsem.at[len(local)])
        copy.start()
        local.append(copy)
        return copy

    up_own = upb.at[x, zl, c]
    got_tok = fetch(tokens.at[0], tok.at[cols(0, 16)])
    got_up = fetch(up_w, up_own)
    got_down = fetch(down_w, dwn.at[cols(0, 256), cols(0, 128)])
    got_p = fetch(params.at[0], pbuf)
    got_t = fetch(tracker.at[0], tbuf)
    got_tgt = []
    for rc in range(2):
        for rx in range(4):
            for rz in range(2):
                who = ((x + rx) % 4) * 4 + ((zl + rz) % 2) * 2 + (c + rc) % 2
                src = targets.at[0, :, pl.ds(pl.multiple_of(who * 128, 128), 128)]
                got_tgt.append(fetch(src, tgt.at[:, cols(rc * 1024 + rx * 256 + rz * 128, 128)]))

    barrier = pltpu.get_barrier_semaphore()
    peers = [other_core, off_chip, other_z, beyond, along_x(1), along_x(-1)]
    peers += [along_y(r) for r in range(1, 8)] + [along_z(1), along_z(-1)]
    for peer in peers:
        pl.semaphore_signal(barrier, inc=1, device_id=peer, device_id_type=MESH)
    pl.semaphore_wait(barrier, len(peers))

    sent = []

    def message(src, dst, peer, k, out=None):
        out = k if out is None else out
        return pltpu.make_async_remote_copy(
            src_ref=src, dst_ref=dst, send_sem=ssem.at[out], recv_sem=rsem.at[k],
            device_id=peer, device_id_type=MESH,
        )

    def send(src, dst, peer, k):
        copy = message(src, dst, peer, k)
        copy.start()
        sent.append(copy)

    def arrive(dst, k):
        message(dst, dst, other_core, k).wait_recv()

    def tok_at(r, q):
        return tok.at[cols((r % 8) * 64 + (q % 4) * 16, 16)]

    def dwn_at(r, rx, first=0, rows=256):
        return dwn.at[cols((r % 8) * 256 + first, rows), cols(rx * 256, 256)]

    def tok_steps(way, q):
        return 4 if (q < 2) == (way == 0) else 3

    def tok_step(way, s, q):
        sign = 1 if way == 0 else -1
        send(tok_at(-sign * (s - 1), q), tok_at(-sign * s, q), along_y(sign), TY(way, s, q))

    def tok_wait(way, s, q):
        sign = 1 if way == 0 else -1
        arrive(tok_at(-sign * s, q), TY(way, s, q))

    def dwn_rows(way, s):
        return (0, NEAR) if s < 4 else (NEAR // 2 * way, NEAR // 2)

    def dwn_step(way, s):
        sign = 1 if way == 0 else -1
        part = dwn_rows(way, s)
        send(
            dwn_at(-sign * (s - 1), 0, *part), dwn_at(-sign * s, 0, *part),
            along_y(sign), DY(way, s),
        )

    def dwn_wait(way, s):
        sign = 1 if way == 0 else -1
        arrive(dwn_at(-sign * s, 0, *dwn_rows(way, s)), DY(way, s))

    def dwn_piece(r, z):
        return dwn.at[cols((r % 8) * 256, NEAR), cols(z * 128, 128)]

    def far_at(r, way, s):
        first, n = (NEAR, 256 - NEAR) if s < 4 else (NEAR + (256 - NEAR) // 2 * way, (256 - NEAR) // 2)
        return dwn.at[cols((r % 8) * 256 + first, n), cols(0, 1024)]

    def far_step(way, s):
        sign = 1 if way == 0 else -1
        send(
            far_at(-sign * (s - 1), way, s), far_at(-sign * s, way, s), along_y(sign), EY(way, s)
        )

    def far_wait(s):
        for way in range(2):
            sign = 1 if way == 0 else -1
            arrive(far_at(-sign * s, way, s), EY(way, s))
            if s < 4:
                far_step(way, s + 1)

    def x_first(r):
        send(dwn_at(r, 0, 0, NEAR), dwn_at(r, 3, 0, NEAR), along_x(1), DX(0, r))
        send(dwn_at(r, 0, 0, NEAR), dwn_at(r, 1, 0, NEAR), along_x(-1), DX(1, r))

    def x_pieces(r):
        n = (256 if r == 0 else NEAR) // 2
        return (0, n), (n, n)

    def x_second(r):
        if r == 0:
            for way, rx in ((0, 3), (1, 1)):
                arrive(dwn.at[cols(0, 256), cols(rx * 256, 128)], D0(way))
                arrive(dwn.at[cols(0, 256), cols(rx * 256 + 128, 128)], DX(way, 0))
        else:
            arrive(dwn_at(r, 3, 0, NEAR), DX(0, r))
            arrive(dwn_at(r, 1, 0, NEAR), DX(1, r))
        low, high = x_pieces(r)
        send(dwn_at(r, 3, *low), dwn_at(r, 2, *low), along_x(1), DF(0, r))
        send(dwn_at(r, 1, *high), dwn_at(r, 2, *high), along_x(-1), DF(1, r))

    def core_half(r, rc):
        return dwn.at[cols((r % 8) * 256, 256), cols(rc * 1024, 1024)]

    def x_third(r):
        for way in range(2):
            arrive(dwn_at(r, 2, *x_pieces(r)[way]), DF(way, r))
        send(core_half(r, 0), core_half(r, 1), other_core, DC(r))

    def half_cols(way):
        return cols(way * 1024, 1024)

    def ring_z(ref, base, first):
        own, below, above, far = (ref.at[cols(base + 16 * k, 16)] for k in (0, 3, 1, 2))

        def start():
            send(own, below, along_z(1), first(0, 0))
            send(own, above, along_z(-1), first(0, 1))

        def forward():
            arrive(below, first(0, 0))
            send(below.at[:, half_cols(0)], far.at[:, half_cols(0)], along_z(1), first(1, 0))
            arrive(above, first(0, 1))
            send(above.at[:, half_cols(1)], far.at[:, half_cols(1)], along_z(-1), first(1, 1))

        def finish():
            for way in range(2):
                arrive(far.at[:, half_cols(way)], first(1, way))

        return start, forward, finish

    tok_start, tok_forward, tok_finish = ring_z(tok, 0, TZ)
    got_tok.wait()
    tok_start()
    for way in range(2):
        tok_step(way, 1, 0)
    got_down.wait()
    own_down = dwn.at[cols(0, 256), cols(0, 128)]
    send(own_down, dwn.at[cols(0, 256), cols(128, 128)], other_z, DZ(0))
    for way, rx in ((0, 3), (1, 1)):
        send(own_down, dwn.at[cols(0, 256), cols(rx * 256, 128)], along_x(1 - 2 * way), D0(way))
        send(dwn_piece(0, 0), dwn_piece(2 * way - 1, 0), along_y(1 - 2 * way), DB(way))
    got_up.wait()
    send(up_own, up_own, other_z, UZ(0))
    got_p.wait()
    send(pbuf, pin, other_core, PI(0))
    got_t.wait()
    send(tbuf, tin, other_core, TI(0))

    tok_forward()
    for way in range(2):
        tok_step(way, 1, 3)
        tok_step(way, 1, 1)
    z_down = dwn.at[cols(0, 256), cols(128, 128)]
    arrive(z_down, DZ(0))
    for way, rx in ((0, 3), (1, 1)):
        send(z_down, dwn.at[cols(0, 256), cols(rx * 256 + 128, 128)], along_x(1 - 2 * way), DX(way, 0))
        send(dwn_piece(0, 1), dwn_piece(2 * way - 1, 1), along_y(1 - 2 * way), DY(way, 1))
    arrive(upb.at[x, 1 - zl, c], UZ(0))
    send(upb.at[x, :, c], upb.at[x, :, c], along_x(1), UX(0))
    send(upb.at[x, :, c], upb.at[x, :, c], along_x(-1), UX(1))
    tok_finish()
    for way in range(2):
        tok_step(way, 1, 2)

    low, high = cols(0, 1024), cols(1024, 1024)

    @pl.when(diagonal)
    def _():
        message(pbuf.at[high], prel, other_z, PR(0)).start()
        message(pbuf.at[low], pof.at[low], off_chip, PO(0)).start()

    @pl.when(jnp.logical_not(diagonal))
    def _():
        message(pbuf.at[low], pof.at[low], off_chip, PO(0)).start()
        message(pbuf.at[high], pof.at[high], off_chip, PO(1)).start()

    for copy in got_tgt:
        copy.wait()

    for s in range(1, 5):
        for way in range(2):
            if s == 1:
                arrive(dwn_piece(2 * way - 1, 0), DB(way))
                arrive(dwn_piece(2 * way - 1, 1), DY(way, 1))
            else:
                dwn_wait(way, s)
            if s < 4:
                dwn_step(way, s + 1)
        for r in (8 - s, s)[: 2 if s < 4 else 1]:
            x_first(r)
        for q in (0, 3, 1, 2):
            for way in range(2):
                if s <= tok_steps(way, q):
                    tok_wait(way, s, q)
                    if s < tok_steps(way, q):
                        tok_step(way, s + 1, q)
        if s == 1:
            x_second(0)
            below, above = (x + 3) % 4, (x + 1) % 4
            arrive(upb.at[below, :, c], UX(0))
            send(upb.at[below, 0, c], upb.at[below, 0, c], along_x(1), UF(0))
            arrive(upb.at[above, :, c], UX(1))
            send(upb.at[above, 1, c], upb.at[above, 1, c], along_x(-1), UF(1))
        if s == 2:
            x_third(0)
            for way in range(2):
                far_step(way, 1)
        if s == 3:
            far_wait(1)
            across = (x + 2) % 4
            arrive(upb.at[across, 0, c], UF(0))
            arrive(upb.at[across, 1, c], UF(1))
            send(upb.at[:, :, c], upb.at[:, :, c], other_core, UC(0))
            x_second(7)
            x_second(1)

            @pl.when(jnp.logical_not(diagonal))
            def _():
                arrive(prel, PR(0))
                message(prel, pof.at[high], beyond, PO(1), PO(2)).start()

        if s == 4:
            far_wait(2)
            x_second(6)
            x_second(2)

    @pl.when(diagonal)
    def _():
        message(tbuf, trel, other_z, TR(0)).start()

    @pl.when(jnp.logical_not(diagonal))
    def _():
        message(tbuf, tof, off_chip, TO(0)).start()

    def rows256(i):
        return pl.ds(pl.multiple_of(i * 256, 256), 256)

    arrive(upb.at[:, :, 1 - c], UC(0))

    @pl.loop(0, 2)
    def _(i):
        rows = rows256(i)
        total = jnp.zeros((256, 256), F32)
        for k in range(8):
            total += jnp.dot(
                tok[rows, k * 256 : (k + 1) * 256],
                upb[k // 2, k % 2].reshape(256, 256),
                preferred_element_type=F32,
            )
        upv[rows, :] = total

    def hidden_of(p, weights):
        @pl.loop(0, 2)
        def _(i):
            rows = rows256(i)
            gate = jnp.dot(tok[rows, :], weights[...], preferred_element_type=F32) * scale
            sig = jax.nn.sigmoid(gate)
            up = upv[rows, :]
            hsend[p, rows, :] = (sig * gate * up).astype(BF16)
            fac[p, rows, :] = up * sig * (1.0 + gate * (1.0 - sig))

        for r in FAR_FIRST:
            send(
                hsend.at[p, cols(r * 64, 64)], hall.at[p, :, cols((8 - r) * 256, 256)],
                along_y(r), HI(p, r),
            )
        hall[p, :, 0:256] = hsend[p, 0:64, :]

    hidden_of(0, pbuf)
    far_wait(3)
    x_second(5)
    x_second(3)
    x_third(7)
    x_third(1)
    x_second(4)

    e_off = edge[(a + c + 15) % 16]
    e_in = edge[(a + 16 - c) % 16]
    own = 1.0 - e_off - e_in
    eta = step[0]
    arrive(pin, PI(0))
    arrive(pof.at[low], PO(0))
    arrive(pof.at[high], PO(1))

    @pl.loop(0, 8)
    def _(i):
        rows = rows256(i)
        mixed = own * pbuf[rows, :].astype(F32)
        mixed += e_off * pof[rows, :].astype(F32) + e_in * pin[rows, :].astype(F32)
        fresh[rows, :] = (mixed - eta * tbuf[rows, :].astype(F32)).astype(BF16)

    fresh_copy = pltpu.make_async_copy(fresh, fresh_out.at[0], lsem.at[len(local)])
    fresh_copy.start()
    hidden_of(1, fresh)
    x_third(6)
    x_third(2)
    far_wait(4)
    x_third(5)
    x_third(3)
    x_third(4)

    @pl.when(jnp.logical_not(diagonal))
    def _():
        arrive(trel, TR(0))
        message(trel, tof, beyond, TO(0), TO(1)).start()

    for r in ORDER:
        arrive(core_half(r, 1), DC(r))

    def sum_first(p, way):
        rows, part = cols(32, 16), half_cols(way)
        return psend.at[p, rows, part], pmid.at[p, :, part]

    def sum_second(p, way, half):
        rows, part = cols(16 + 32 * way, 16), half_cols(half)
        return psend.at[p, rows, part], prec.at[p, way, :, part]

    def partial_of(p):
        for r in FAR_FIRST:
            arrive(hall.at[p, :, cols((8 - r) * 256, 256)], HI(p, r))

        @pl.loop(0, 8)
        def _(i):
            part = jnp.dot(hall[p], dwn[:, rows256(i)], preferred_element_type=F32)
            psend[p, :, rows256(i)] = part.astype(BF16)

        for way in range(2):
            send(*sum_first(p, way), along_z(1 - 2 * way), RS(p, 0, way))
        for way in range(2):
            send(*sum_second(p, way, 1 - way), along_z(1 - 2 * way), RS(p, 1, way))

    def middle_of(p):
        for way in range(2):
            arrive(sum_first(p, way)[1], RS(p, 0, way))
            rows, part = cols(16 + 32 * way, 16), half_cols(way)
            both = psend[p, rows, part].astype(F32) + pmid[p, :, part].astype(F32)
            psend[p, rows, part] = both.astype(BF16)
            send(*sum_second(p, way, way), along_z(1 - 2 * way), RS(p, 2, way))

    err_ring = [ring_z(eall.at[p], 0, functools.partial(EG, p)) for p in range(2)]

    def err_of(p):
        total = psend[p, 0:16, :].astype(F32)
        for way in range(2):
            for half in range(2):
                arrive(sum_second(p, way, half)[1], RS(p, 2 if half == way else 1, way))
            total += prec[p, way].astype(F32)
        eall[p, 0:16, :] = (2.0 * (total - tgt[...].astype(F32))).astype(BF16)
        err_ring[p][0]()

    partial_of(0)
    partial_of(1)
    middle_of(0)
    middle_of(1)
    err_of(0)
    err_of(1)
    for p in range(2):
        err_ring[p][1]()

    def back_block(p, r):
        return lax.dot_general(
            eall[p], dwn[pl.ds(pl.multiple_of(r * 256, 256), 256), :],
            (((1,), (1,)), ((), ())), preferred_element_type=F32,
        ).astype(BF16)

    def back_message(p, r):
        rows = pl.ds(pl.multiple_of(r * 64, 64), 64)
        land = pl.ds(pl.multiple_of((8 - r) * 64, 64), 64)
        return message(bsend.at[p, rows], brec.at[p, land], along_y(r), BK(p, 0) + r)

    def back_of(p):
        err_ring[p][2]()

        @pl.loop(0, 7)
        def _(k):
            r = 4 + ((k + 1) // 2) * (1 - 2 * (k % 2))
            bsend[p, pl.ds(pl.multiple_of(r * 64, 64), 64), :] = back_block(p, r)
            back_message(p, r).start()

        brec[p, 0:64, :] = back_block(p, 0)

    back_of(0)
    back_of(1)

    arrive(tin, TI(0))
    arrive(tof, TO(0))

    @pl.loop(0, 8)
    def _(i):
        rows = rows256(i)
        turned[rows, :] = tok[:, rows].T
        mixed = own * tbuf[rows, :].astype(F32)
        mixed += e_off * tof[rows, :].astype(F32) + e_in * tin[rows, :].astype(F32)
        mixed_y[rows, :] = mixed

    for p in range(2):

        @pl.loop(1, 8)
        def _(r):
            land = pl.ds(pl.multiple_of((8 - r) * 64, 64), 64)
            message(brec.at[p, land], brec.at[p, land], other_core, BK(p, 0) + r).wait_recv()

    dd[...] = (
        brec[1].astype(F32) * fac[1] - brec[0].astype(F32) * fac[0]
    ).astype(BF16)

    @pl.loop(0, 8)
    def _(i):
        rows = rows256(i)
        change = jnp.dot(turned[rows, :], dd[...], preferred_element_type=F32)
        trk[rows, :] = (mixed_y[rows, :] + change * scale).astype(BF16)
        pltpu.make_async_copy(trk.at[rows], track_out.at[0, rows], lsem.at[len(local) + 1]).start()

    for copy in sent:
        copy.wait_send()

    @pl.when(diagonal)
    def _():
        message(pbuf.at[high], prel, other_z, PR(0)).wait_send()
        message(pbuf.at[low], pof.at[low], off_chip, PO(0)).wait_send()
        message(tbuf, trel, other_z, TR(0)).wait_send()

    @pl.when(jnp.logical_not(diagonal))
    def _():
        message(pbuf.at[low], pof.at[low], off_chip, PO(0)).wait_send()
        message(pbuf.at[high], pof.at[high], off_chip, PO(1)).wait_send()
        message(prel, pof.at[high], beyond, PO(1), PO(2)).wait_send()
        message(tbuf, tof, off_chip, TO(0)).wait_send()
        message(trel, tof, beyond, TO(0), TO(1)).wait_send()

    for p in range(2):

        @pl.loop(1, 8)
        def _(r):
            back_message(p, r).wait_send()

    fresh_copy.wait()
    pltpu.make_async_copy(trk, track_out.at[0], lsem.at[len(local) + 1]).wait()


def on_device(tokens, targets, params, tracker, up_weight, down_weight, edge_weight, step_size):
    hbm = pl.BlockSpec(memory_space=pltpu.HBM)
    smem = pl.BlockSpec(memory_space=pltpu.SMEM)
    block = pltpu.VMEM((2048, 256), BF16)
    out = jax.ShapeDtypeStruct(params.shape, BF16)
    return pl.pallas_call(
        kernel,
        out_shape=(out, out),
        in_specs=[smem, smem] + [hbm] * 6,
        out_specs=(hbm, hbm),
        scratch_shapes=[
            pltpu.VMEM((512, 2048), BF16),
            pltpu.VMEM((16, 2048), BF16),
            block, block, block, block, block, block, block,
            pltpu.VMEM((4, 2, 2, 128, 256), BF16),
            pltpu.VMEM((2048, 2048), BF16),
            pltpu.VMEM((512, 256), F32),
            pltpu.VMEM((2, 512, 256), F32),
            pltpu.VMEM((2, 512, 256), BF16),
            pltpu.VMEM((2, 64, 2048), BF16),
            pltpu.VMEM((2, 64, 2048), BF16),
            pltpu.VMEM((2, 16, 2048), BF16),
            pltpu.VMEM((2, 2, 16, 2048), BF16),
            pltpu.VMEM((2, 64, 2048), BF16),
            pltpu.VMEM((2, 512, 256), BF16),
            pltpu.VMEM((2, 512, 256), BF16),
            pltpu.VMEM((512, 256), BF16),
            block,
            pltpu.VMEM((1024, 256), BF16),
            block,
            pltpu.VMEM((2048, 512), BF16),
            pltpu.VMEM((2048, 256), F32),
            pltpu.SemaphoreType.DMA((SEMS,)),
            pltpu.SemaphoreType.DMA((SEMS,)),
            pltpu.SemaphoreType.DMA((24,)),
        ],
        compiler_params=pltpu.CompilerParams(
            collective_id=0, has_side_effects=True, vmem_limit_bytes=56 * 1024 * 1024
        ),
    )(edge_weight, step_size, tokens, targets, params, tracker, up_weight, down_weight)


def solution(mesh):
    in_specs = (
        P("agent", "tp", None),
        P("agent", "tp", None),
        P("agent", None, "tp"),
        P("agent", None, "tp"),
        P("agent", "tp"),
        P("tp", "agent"),
        P(),
        P(),
    )
    out_specs = (P("agent", None, "tp"), P("agent", None, "tp"))
    return jax.shard_map(
        on_device, mesh=mesh, in_specs=in_specs, out_specs=out_specs, check_vma=False
    )
```

time: 132 us -> 117 us (0.89)
  Pallas kernels: 127 us -> 113 us
    pallas_call x1, Pallas kernels: 127 us -> 113 us  [on_device(): pl.pallas_call(kernel, out_shape=(out, out), in_specs=[smem, smem] + [hbm...]
where the time goes in v2:
time: 117 us
  Pallas kernels  113 us (97%)
  local copies, waits for them, and re-layouts  3.32 us (3%)
  between operations  1.3 us (1%)
    pallas_call x1, Pallas kernels, on_device(): pl.pallas_call(kernel, out_shape=(out, out), in_specs=[smem, smem] + [hbm...  113 us
    unnamed x4, local copies, waits for them, and re-layouts  3.32 us

profile of v2, /device:TPU:1, one launch (start us, length us, event | category | flops | bytes accessed | tf_op | source)
XLA Modules:
  0.0 117.3 jit_solution(16485851689870864138)
XLA Ops:
  1.3 112.6 %shard_map.95 = (bf16[1,2048,256]{2,1,0:T(8,128)(2,1)}, bf16[1,2048,256]{2,1,0:T(8,128)(2,1)}) custom-call(f32[16]{0:T(128)} %edge.1, f32[1]{0:T(128)S(6)} %copy.12.step, bf16[1,16,2048]{2,1,0:T(8,128)(2,1)} %tokens.1, bf16[1,16,2048]{2,1,0:T(8,128)(2,1)} %targets.1, bf16[1,2048,256]{2,1,0:T(8,128)(2,1)} %params.1, bf16[1,2048,256]{2,1,0:T(8,128)(2,1)} %tracker.1, ...), custom_call_target="tpu_custom_call" | custom-call | tf_op jit(solution)/shard_map/pallas_call | solution.py:544
  113.9 0.0 copy-start
  113.9 2.4 %copy.13 = bf16[1,2048,256]{2,1,0:T(8,128)(2,1)} copy(bf16[1,2048,256]{2,1,0:T(8,128)(2,1)} %get-tuple-element.4) | data formatting | bytes 2097152
  116.3 0.0 copy-done
  116.3 1.0 copy.14
Async XLA Ops:
  113.9 2.4 %copy-start = (bf16[1,2048,256]{2,1,0:T(8,128)(2,1)S(1)}, bf16[1,2048,256]{2,1,0:T(8,128)(2,1)}, u32[]{:S(2)}) copy-start(bf16[1,2048,256]{2,1,0:T(8,128)(2,1)} %get-tuple-element.5) | copy-start | bytes 3145732

commit v3 on v2

v3 whole, which is shorter than its diff:
```python
import functools
import math

import jax
import jax.numpy as jnp
from jax import lax
from jax.experimental import pallas as pl
from jax.experimental.pallas import tpu as pltpu
from jax.sharding import PartitionSpec as P

MESH = pl.DeviceIdType.MESH
BF16 = jnp.bfloat16
F32 = jnp.float32
ORDER = (0, 7, 1, 6, 2, 5, 3, 4)
NEAR = 224
PARTS = 4
FAR_FIRST = (4, 3, 5, 2, 6, 1, 7)


class Plan:
    def __init__(self):
        self.count = 0

    def take(self, *shape):
        size = 1
        for n in shape:
            size *= n
        base = self.count
        self.count += size

        def number(*index):
            flat = 0
            for i, n in zip(index, shape):
                flat = flat * n + i
            return base + flat

        return number


plan = Plan()
TZ, TY = plan.take(3), plan.take(2, 2, 7)
UZ, UX, UF, UC = plan.take(1), plan.take(2), plan.take(1), plan.take(1)
DZ, DB, D0 = plan.take(1), plan.take(2), plan.take(2)
DY, EY = plan.take(2, 4), plan.take(2, 4)
DX, DF, DC = plan.take(2, 8), plan.take(8), plan.take(8)
PI, PO, TI, TO, PR = plan.take(1), plan.take(3), plan.take(1), plan.take(1), plan.take(2)
HI, BK = plan.take(2), plan.take(2)
RS, EG = plan.take(2, 3), plan.take(2, 3)
SEMS = plan.count
SENDS = 8
BLOCK_SENT, ON_SENT, STRAIGHT_SENT, BACK_SENT = range(SENDS, SENDS + 4)

def kernel(
    edge, step, tokens, targets, params, tracker, up_w, down_w, fresh_out, dd_out, turned_out, mixed_out,
    tok, tgt, pbuf, tbuf, pin, pof, tin, tof, fresh, upb, dwn, upv, fac, hsend, hall,
    psend, pmid, prec, eall, bsend, brec, dd, prel, turned, mixed_y, ssem, rsem, lsem,
):
    a = lax.axis_index("agent")
    t = lax.axis_index("tp")
    x, zl, c = a // 4, (a // 2) % 2, a % 2
    zh, y = t // 8, t % 8
    scale = 2048.0 ** -0.5

    def along_y(r):
        return (a, zh * 8 + (y + r + 8) % 8)

    def along_z(q):
        return (a, ((zh + q + 4) % 4) * 8 + y)

    def along_x(r):
        return ((a + 4 * r + 16) % 16, t)

    other_core = (a + 1 - 2 * c, t)
    off_chip = ((a + 2 * c + 15) % 16, t)
    other_z = (a + 2 - 4 * zl, t)
    onward = ((a + 8 * c + 12) % 16, t)
    corner = (4 * x + 3 - (a % 4), t)
    diagonal = c == zl

    def cols(first, n):
        return pl.ds(first, n)

    def fetch(src, dst, k):
        copy = pltpu.make_async_copy(src, dst, lsem.at[k])
        copy.start()
        return copy

    up_own = upb.at[x, zl, c]
    got_tok = fetch(tokens.at[0], tok.at[cols(0, 16)], 0)
    got_up = fetch(up_w, up_own, 1)
    got_down = fetch(down_w, dwn.at[cols(0, 256), cols(0, 128)], 2)
    got_p = fetch(params.at[0], pbuf, 3)
    got_t = fetch(tracker.at[0], tbuf, 4)
    for rc in range(2):
        for rx in range(4):
            for rz in range(2):
                who = ((x + rx) % 4) * 4 + ((zl + rz) % 2) * 2 + (c + rc) % 2
                src = targets.at[0, :, pl.ds(pl.multiple_of(who * 128, 128), 128)]
                fetch(src, tgt.at[:, cols(rc * 1024 + rx * 256 + rz * 128, 128)], 5)

    barrier = pltpu.get_barrier_semaphore()
    peers = [other_core, off_chip, other_z, corner, along_x(1), along_x(-1)]
    peers += [along_y(r) for r in range(1, 8)] + [along_z(1), along_z(-1)]
    for peer in peers:
        pl.semaphore_signal(barrier, inc=1, device_id=peer, device_id_type=MESH)
    pl.semaphore_wait(barrier, len(peers))

    sent = [0]

    def message(src, dst, peer, k, out=0):
        return pltpu.make_async_remote_copy(
            src_ref=src, dst_ref=dst, send_sem=ssem.at[out], recv_sem=rsem.at[k],
            device_id=peer, device_id_type=MESH,
        )

    def send(src, dst, peer, k):
        message(src, dst, peer, k, len(sent) - 1).start()
        sent[-1] += math.prod(src.shape) * 2
        if sent[-1] >= 5 << 19 and sent[-1] % (1 << 15) == 0:
            sent.append(0)

    def arrive(dst, k):
        message(dst, dst, other_core, k).wait_recv()

    def all_sent(nbytes, out):
        rows = dwn.at[cols(0, nbytes // 2048), cols(0, 1024)]
        message(rows, rows, other_core, 0, out).wait_send()

    def tok_at(r, q):
        return tok.at[cols((r % 8) * 64 + (q % 4) * 16, 16)]

    def dwn_at(r, rx, first=0, rows=256):
        return dwn.at[cols((r % 8) * 256 + first, rows), cols(rx * 256, 256)]

    def tok_steps(way, q):
        return 4 if (q < 2) == (way == 0) else 3

    def tok_sem(way, s, q):
        pair, rank = divmod(q, 2)
        if pair == way:
            return TY(way, rank, s - 1)
        return TY(way, rank, 3 + s)

    def tok_step(way, s, q):
        sign = 1 if way == 0 else -1
        send(tok_at(-sign * (s - 1), q), tok_at(-sign * s, q), along_y(sign), tok_sem(way, s, q))

    def tok_wait(way, s, q):
        sign = 1 if way == 0 else -1
        arrive(tok_at(-sign * s, q), tok_sem(way, s, q))

    def dwn_rows(way, s):
        return (0, NEAR) if s < 4 else (NEAR // 2 * way, NEAR // 2)

    def dwn_step(way, s):
        sign = 1 if way == 0 else -1
        part = dwn_rows(way, s)
        send(
            dwn_at(-sign * (s - 1), 0, *part), dwn_at(-sign * s, 0, *part),
            along_y(sign), DY(way, s - 1),
        )

    def dwn_wait(way, s):
        sign = 1 if way == 0 else -1
        arrive(dwn_at(-sign * s, 0, *dwn_rows(way, s)), DY(way, s - 1))

    def dwn_piece(r, z):
        return dwn.at[cols((r % 8) * 256, NEAR), cols(z * 128, 128)]

    def far_at(r, way, s):
        first, n = (NEAR, 256 - NEAR) if s < 4 else (NEAR + (256 - NEAR) // 2 * way, (256 - NEAR) // 2)
        return dwn.at[cols((r % 8) * 256 + first, n), cols(0, 1024)]

    def far_step(way, s):
        sign = 1 if way == 0 else -1
        send(
            far_at(-sign * (s - 1), way, s), far_at(-sign * s, way, s), along_y(sign), EY(way, s - 1)
        )

    def far_wait(s):
        for way in range(2):
            sign = 1 if way == 0 else -1
            arrive(far_at(-sign * s, way, s), EY(way, s - 1))
            if s < 4:
                far_step(way, s + 1)

    def x_first(r):
        send(dwn_at(r, 0, 0, NEAR), dwn_at(r, 3, 0, NEAR), along_x(1), DX(0, r))
        send(dwn_at(r, 0, 0, NEAR), dwn_at(r, 1, 0, NEAR), along_x(-1), DX(1, r))

    def x_pieces(r):
        n = (256 if r == 0 else NEAR) // 2
        return (0, n), (n, n)

    def x_second(r):
        if r == 0:
            for way, rx in ((0, 3), (1, 1)):
                arrive(dwn.at[cols(0, 256), cols(rx * 256, 128)], D0(way))
                arrive(dwn.at[cols(0, 256), cols(rx * 256 + 128, 128)], DX(way, 0))
        else:
            arrive(dwn_at(r, 3, 0, NEAR), DX(0, r))
            arrive(dwn_at(r, 1, 0, NEAR), DX(1, r))
        low, high = x_pieces(r)
        send(dwn_at(r, 3, *low), dwn_at(r, 2, *low), along_x(1), DF(r))
        send(dwn_at(r, 1, *high), dwn_at(r, 2, *high), along_x(-1), DF(r))

    def core_half(r, rc):
        return dwn.at[cols((r % 8) * 256, 256), cols(rc * 1024, 1024)]

    def x_third(r):
        arrive(dwn_at(r, 2, 0, 256 if r == 0 else NEAR), DF(r))
        send(core_half(r, 0), core_half(r, 1), other_core, DC(r))

    def half_cols(way):
        return cols(way * 1024, 1024)

    def ring_z(ref, base, first):
        own, below, above, far = (ref.at[cols(base + 16 * k, 16)] for k in (0, 3, 1, 2))

        def start():
            send(own, below, along_z(1), first(0))
            send(own, above, along_z(-1), first(1))

        def forward():
            arrive(below, first(0))
            send(below.at[:, half_cols(0)], far.at[:, half_cols(0)], along_z(1), first(2))
            arrive(above, first(1))
            send(above.at[:, half_cols(1)], far.at[:, half_cols(1)], along_z(-1), first(2))

        def finish():
            arrive(far, first(2))

        return start, forward, finish

    tok_start, tok_forward, tok_finish = ring_z(tok, 0, TZ)
    got_down.wait()
    own_down = dwn.at[cols(0, 256), cols(0, 128)]
    send(own_down, dwn.at[cols(0, 256), cols(128, 128)], other_z, DZ(0))
    got_tok.wait()
    tok_start()
    for way in range(2):
        tok_step(way, 1, 0)
    for way, rx in ((0, 3), (1, 1)):
        send(own_down, dwn.at[cols(0, 256), cols(rx * 256, 128)], along_x(1 - 2 * way), D0(way))
        send(dwn_piece(0, 0), dwn_piece(2 * way - 1, 0), along_y(1 - 2 * way), DB(way))
    got_up.wait()
    send(up_own, up_own, other_z, UZ(0))
    got_p.wait()
    low, quarters = cols(0, 1024), (cols(1024, 512), cols(1536, 512))

    def onward_half(k):
        return message(pbuf.at[quarters[k]], prel.at[cols(512 * k, 512)], onward, PR(k), ON_SENT)

    def corner_half(k):
        return message(prel.at[cols(512 * k, 512)], pof.at[quarters[k]], corner, PO(1 + k), ON_SENT)

    def straight_half(k):
        return message(pbuf.at[quarters[k]], pof.at[quarters[k]], off_chip, PO(1 + k), STRAIGHT_SENT)

    direct_half = message(pbuf.at[low], pof.at[low], off_chip, PO(0), BLOCK_SENT)

    @pl.when(diagonal)
    def _():
        onward_half(0).start()

    send(pbuf, pin, other_core, PI(0))
    got_t.wait()
    send(tbuf, tin, other_core, TI(0))

    z_down = dwn.at[cols(0, 256), cols(128, 128)]
    arrive(z_down, DZ(0))
    for way, rx in ((0, 3), (1, 1)):
        send(dwn_piece(0, 1), dwn_piece(2 * way - 1, 1), along_y(1 - 2 * way), DY(way, 0))
        send(z_down, dwn.at[cols(0, 256), cols(rx * 256 + 128, 128)], along_x(1 - 2 * way), DX(way, 0))
    tok_forward()
    for way in range(2):
        tok_step(way, 1, 3)
        tok_step(way, 1, 1)

    arrive(upb.at[x, 1 - zl, c], UZ(0))
    send(upb.at[x, :, c], upb.at[x, :, c], along_x(1), UX(0))
    send(upb.at[x, :, c], upb.at[x, :, c], along_x(-1), UX(1))

    @pl.when(jnp.logical_not(diagonal))
    def _():
        direct_half.start()
        straight_half(0).start()
        straight_half(1).start()

    tok_finish()
    for way in range(2):
        tok_step(way, 1, 2)
    pltpu.make_async_copy(tgt, tgt, lsem.at[5]).wait()

    def down(s):
        for way in range(2):
            if s == 1:
                arrive(dwn_piece(2 * way - 1, 0), DB(way))
                arrive(dwn_piece(2 * way - 1, 1), DY(way, 0))
            else:
                dwn_wait(way, s)
            if s < 4:
                dwn_step(way, s + 1)
        if s == 1:
            x_second(0)
        for r in (8 - s, s)[: 2 if s < 4 else 1]:
            x_first(r)

    def token(s, *pieces):
        for q in pieces:
            for way in range(2):
                if s <= tok_steps(way, q):
                    tok_wait(way, s, q)
                    if s < tok_steps(way, q):
                        tok_step(way, s + 1, q)

    down(1)
    token(1, 0, 3)
    down(2)
    whole_t = message(tbuf, tof, off_chip, TO(0), BLOCK_SENT)

    @pl.when(jnp.logical_not(diagonal))
    def _():
        whole_t.start()

    def track_piece(k):
        rows = cols(1024 * k, 1024)

        @pl.when(diagonal)
        def _():
            message(tbuf.at[rows], tof.at[rows], off_chip, TO(0), BLOCK_SENT).start()

    below, above, across = (x + 3) % 4, (x + 1) % 4, (x + 2) % 4
    arrive(upb.at[below, :, c], UX(0))
    send(upb.at[below, 0, c], upb.at[below, 0, c], along_x(1), UF(0))
    arrive(upb.at[above, :, c], UX(1))
    send(upb.at[above, 1, c], upb.at[above, 1, c], along_x(-1), UF(0))
    token(1, 1, 2)

    @pl.when(diagonal)
    def _():
        onward_half(1).start()
        arrive(prel.at[cols(0, 512)], PR(0))
        corner_half(0).start()

    token(2, 0)
    x_third(0)
    for way in range(2):
        far_step(way, 1)
    down(3)

    @pl.when(diagonal)
    def _():
        direct_half.start()

    token(2, 3, 1)
    x_second(7)
    x_second(1)
    down(4)
    token(2, 2)
    far_wait(1)

    @pl.when(diagonal)
    def _():
        arrive(prel.at[cols(512, 512)], PR(1))
        corner_half(1).start()

    token(3, 0, 3)
    x_second(6)
    x_second(2)
    arrive(upb.at[across, :, c], UF(0))
    send(upb.at[:, :, c], upb.at[:, :, c], other_core, UC(0))
    token(3, 1, 2)
    far_wait(2)
    x_third(7)
    x_third(1)
    token(4, 0, 3, 1, 2)
    far_wait(3)

    def rows256(i):
        return pl.ds(pl.multiple_of(i * 256, 256), 256)

    arrive(upb.at[:, :, 1 - c], UC(0))

    def hidden_half(p, weights, half):
        rows = cols(256 * half, 256)
        if p == 0:
            sums = jnp.zeros((256, 256), F32)
            for k in range(8):
                sums += jnp.dot(
                    tok[rows, k * 256 : (k + 1) * 256],
                    upb[k // 2, k % 2].reshape(256, 256),
                    preferred_element_type=F32,
                )
            upv[rows, :] = sums
        gate = jnp.dot(tok[rows, :], weights[...], preferred_element_type=F32) * scale
        sig = jax.nn.sigmoid(gate)
        up = upv[rows, :]
        hsend[p, rows, :] = (sig * gate * up).astype(BF16)
        fac[p, rows, :] = up * sig * (1.0 + gate * (1.0 - sig))

    def hidden_of(p, weights):
        for half, blocks in ((1, (4, 5, 6, 7)), (0, (3, 2, 1))):
            hidden_half(p, weights, half)
            for r in blocks:
                send(
                    hsend.at[p, cols(r * 64, 64)], hall.at[p, :, cols((8 - r) * 256, 256)],
                    along_y(r), HI(p),
                )
        hall[p, :, 0:256] = hsend[p, 0:64, :]

    hidden_of(0, pbuf)
    track_piece(0)
    x_second(5)
    x_second(3)
    x_second(4)
    x_third(6)
    x_third(2)

    e_off = edge[(a + c + 15) % 16]
    e_in = edge[(a + 16 - c) % 16]
    own = 1.0 - e_off - e_in
    eta = step[0]
    arrive(pin, PI(0))
    arrive(pof.at[low], PO(0))
    for k in range(2):
        arrive(pof.at[quarters[k]], PO(1 + k))

    @pl.loop(0, 8)
    def _(i):
        rows = rows256(i)
        mixed = own * pbuf[rows, :].astype(F32)
        mixed += e_off * pof[rows, :].astype(F32) + e_in * pin[rows, :].astype(F32)
        fresh[rows, :] = (mixed - eta * tbuf[rows, :].astype(F32)).astype(BF16)

    fresh_copy = pltpu.make_async_copy(fresh, fresh_out.at[0], lsem.at[6])
    fresh_copy.start()
    hidden_of(1, fresh)
    far_wait(4)
    x_third(5)
    x_third(3)
    x_third(4)

    def sum_first(p, way):
        rows, part = cols(32, 16), half_cols(way)
        return psend.at[p, rows, part], pmid.at[p, :, part]

    def sum_second(p, way, half):
        rows, part = cols(16 + 32 * way, 16), half_cols(half)
        return psend.at[p, rows, part], prec.at[p, way, :, part]

    def hidden_wait(p):
        arrive(hall.at[p, :, cols(256, 1792)], HI(p))

    def partial_of(p):
        hidden_wait(p)
        for half in range(2):
            if p == 0 and half == 1:
                for r in ORDER:
                    arrive(core_half(r, 1), DC(r))

            @pl.loop(4 * half, 4 * half + 4)
            def _(i):
                part = jnp.dot(hall[p], dwn[:, rows256(i)], preferred_element_type=F32)
                psend[p, :, rows256(i)] = part.astype(BF16)

            send(*sum_first(p, half), along_z(1 - 2 * half), RS(p, half))
            send(*sum_second(p, 1 - half, half), along_z(2 * half - 1), RS(p, 2))

    def middle_of(p):
        for way in range(2):
            arrive(sum_first(p, way)[1], RS(p, way))
            rows, part = cols(16 + 32 * way, 16), half_cols(way)
            both = psend[p, rows, part].astype(F32) + pmid[p, :, part].astype(F32)
            psend[p, rows, part] = both.astype(BF16)
            send(*sum_second(p, way, way), along_z(1 - 2 * way), RS(p, 2))

    err_ring = [ring_z(eall.at[p], 0, functools.partial(EG, p)) for p in range(2)]

    def err_of(p):
        out = psend[p, 0:16, :].astype(F32)
        arrive(prec.at[p], RS(p, 2))
        for way in range(2):
            out += prec[p, way].astype(F32)
        eall[p, 0:16, :] = (2.0 * (out - tgt[...].astype(F32))).astype(BF16)
        err_ring[p][0]()

    partial_of(0)
    partial_of(1)
    middle_of(0)
    middle_of(1)
    err_of(0)
    err_of(1)
    for p in range(2):
        err_ring[p][1]()
    track_piece(1)

    def back_block(p, r):
        return lax.dot_general(
            eall[p], dwn[pl.ds(pl.multiple_of(r * 256, 256), 256), :],
            (((1,), (1,)), ((), ())), preferred_element_type=F32,
        ).astype(BF16)

    def back_message(p, r):
        rows = pl.ds(pl.multiple_of(r * 64, 64), 64)
        land = pl.ds(pl.multiple_of((8 - r) * 64, 64), 64)
        return message(bsend.at[p, rows], brec.at[p, land], along_y(r), BK(p), BACK_SENT)

    def back_of(p):
        err_ring[p][2]()

        @pl.loop(0, 7)
        def _(k):
            r = 4 + ((k + 1) // 2) * (1 - 2 * (k % 2))
            bsend[p, pl.ds(pl.multiple_of(r * 64, 64), 64), :] = back_block(p, r)
            back_message(p, r).start()

        brec[p, 0:64, :] = back_block(p, 0)

    back_of(0)
    back_of(1)

    arrive(tin, TI(0))
    arrive(tof, TO(0))

    def prepare():
        @pl.loop(0, 8)
        def _(i):
            rows = rows256(i)
            turned[rows, :] = tok[:, rows].T
            mixed = own * tbuf[rows, :].astype(F32)
            mixed += e_off * tof[rows, :].astype(F32) + e_in * tin[rows, :].astype(F32)
            mixed_y[rows, :] = mixed

    prepare()
    turned_copy = pltpu.make_async_copy(turned, turned_out, lsem.at[7])
    mixed_copy = pltpu.make_async_copy(mixed_y, mixed_out, lsem.at[0])
    turned_copy.start()
    mixed_copy.start()

    for p in range(2):
        arrive(brec.at[p, cols(64, 448)], BK(p))

    dd[...] = (
        brec[1].astype(F32) * fac[1] - brec[0].astype(F32) * fac[0]
    ).astype(BF16)

    dd_copy = pltpu.make_async_copy(dd, dd_out, lsem.at[5])
    dd_copy.start()

    for g, nbytes in enumerate(sent):
        if nbytes:
            all_sent(nbytes, g)
    all_sent(3 << 19, BLOCK_SENT)
    all_sent(14 << 15, BACK_SENT)

    @pl.when(diagonal)
    def _():
        all_sent(1 << 20, ON_SENT)

    @pl.when(jnp.logical_not(diagonal))
    def _():
        all_sent(1 << 19, STRAIGHT_SENT)

    fresh_copy.wait()
    turned_copy.wait()
    mixed_copy.wait()
    dd_copy.wait()


def last_kernel(
    dd_in, turned_in, mixed_in, fresh_in, fresh_out, track_out,
    dd, turned, mixed, fresh, track, sem, out_sem,
):
    first = pltpu.make_async_copy(dd_in, dd, sem.at[0])
    first.start()
    pieces = []
    for k in range(PARTS):
        rows = pl.ds(k * (2048 // PARTS), 2048 // PARTS)
        a = pltpu.make_async_copy(turned_in.at[rows], turned.at[rows], sem.at[1 + 2 * k])
        b = pltpu.make_async_copy(mixed_in.at[rows], mixed.at[rows], sem.at[2 + 2 * k])
        a.start()
        b.start()
        pieces.append((rows, a, b))
    middle = pltpu.make_async_copy(fresh_in, fresh, sem.at[1 + 2 * PARTS])
    middle.start()
    done = []
    first.wait()
    for k, (rows, a, b) in enumerate(pieces):
        a.wait()
        b.wait()
        change = jnp.dot(turned[rows, :], dd[...], preferred_element_type=F32)
        track[rows, :] = (mixed[rows, :] + change * 2048.0 ** -0.5).astype(BF16)
        done.append(pltpu.make_async_copy(track.at[rows], track_out.at[0, rows], out_sem.at[k]))
        done[-1].start()
        if k == PARTS - 2:
            middle.wait()
            done.append(pltpu.make_async_copy(fresh, fresh_out, out_sem.at[PARTS]))
            done[-1].start()
    for copy in done:
        copy.wait()


def on_device(tokens, targets, params, tracker, up_weight, down_weight, edge_weight, step_size):
    hbm = pl.BlockSpec(memory_space=pltpu.HBM)
    smem = pl.BlockSpec(memory_space=pltpu.SMEM)
    block = pltpu.VMEM((2048, 256), BF16)
    out = jax.ShapeDtypeStruct(params.shape, BF16)
    fresh, dd, turned, mixed = pl.pallas_call(
        kernel,
        out_shape=(
            out,
            jax.ShapeDtypeStruct((512, 256), BF16),
            jax.ShapeDtypeStruct((2048, 512), BF16),
            jax.ShapeDtypeStruct((2048, 256), F32),
        ),
        in_specs=[smem, smem] + [hbm] * 6,
        out_specs=(hbm, hbm, hbm, hbm),
        scratch_shapes=[
            pltpu.VMEM((512, 2048), BF16),
            pltpu.VMEM((16, 2048), BF16),
            block, block, block, block, block, block, block,
            pltpu.VMEM((4, 2, 2, 128, 256), BF16),
            pltpu.VMEM((2048, 2048), BF16),
            pltpu.VMEM((512, 256), F32),
            pltpu.VMEM((2, 512, 256), F32),
            pltpu.VMEM((2, 512, 256), BF16),
            pltpu.VMEM((2, 64, 2048), BF16),
            pltpu.VMEM((2, 64, 2048), BF16),
            pltpu.VMEM((2, 16, 2048), BF16),
            pltpu.VMEM((2, 2, 16, 2048), BF16),
            pltpu.VMEM((2, 64, 2048), BF16),
            pltpu.VMEM((2, 512, 256), BF16),
            pltpu.VMEM((2, 512, 256), BF16),
            pltpu.VMEM((512, 256), BF16),
            pltpu.VMEM((1024, 256), BF16),
            pltpu.VMEM((2048, 512), BF16),
            pltpu.VMEM((2048, 256), F32),
            pltpu.SemaphoreType.DMA((SENDS + 4,)),
            pltpu.SemaphoreType.DMA((SEMS,)),
            pltpu.SemaphoreType.DMA((8,)),
        ],
        compiler_params=pltpu.CompilerParams(
            collective_id=0, has_side_effects=True, vmem_limit_bytes=56 * 1024 * 1024
        ),
    )(edge_weight, step_size, tokens, targets, params, tracker, up_weight, down_weight)
    return pl.pallas_call(
        last_kernel,
        out_shape=(out, out),
        in_specs=[hbm] * 4,
        out_specs=(hbm, hbm),
        scratch_shapes=[
            pltpu.VMEM((512, 256), BF16),
            pltpu.VMEM((2048, 512), BF16),
            pltpu.VMEM((2048, 256), F32),
            pltpu.VMEM((1, 2048, 256), BF16),
            block,
            pltpu.SemaphoreType.DMA((2 + 2 * PARTS,)),
            pltpu.SemaphoreType.DMA((1 + PARTS,)),
        ],
    )(dd, turned, mixed, fresh)


def solution(mesh):
    in_specs = (
        P("agent", "tp", None),
        P("agent", "tp", None),
        P("agent", None, "tp"),
        P("agent", None, "tp"),
        P("agent", "tp"),
        P("tp", "agent"),
        P(),
        P(),
    )
    out_specs = (P("agent", None, "tp"), P("agent", None, "tp"))
    return jax.shard_map(
        on_device, mesh=mesh, in_specs=in_specs, out_specs=out_specs, check_vma=False
    )
```

time: 117 us -> 110 us (0.940)
  Pallas kernels: 113 us -> 109 us
  local copies, waits for them, and re-layouts: 3.32 us -> 0 us
    pallas_call x1 -> x2, Pallas kernels: 113 us -> 109 us  [the longest x1 105 us: on_device(): pl.pallas_call(kernel, out_shape=(out, jax.ShapeDtypeStruct((512, 256), B...]
    unnamed x4 -> x0, local copies, waits for them, and re-layouts: 3.32 us -> none
where the time goes in v3:
time: 110 us
  Pallas kernels  109 us (99%)
  between operations  1.29 us (1%)
    pallas_call x1, Pallas kernels, on_device(): pl.pallas_call(kernel, out_shape=(out, jax.ShapeDtypeStruct((512, 256), B...  105 us
    pallas_call x1, Pallas kernels, on_device(): pl.pallas_call(last_kernel, out_shape=(out, out), in_specs=[hbm] * 4, out...  3.84 us

profile of v3, /device:TPU:1, one launch (start us, length us, event | category | flops | bytes accessed | tf_op | source)
XLA Modules:
  0.0 110.3 jit_solution(15295480259530096076)
XLA Ops:
  1.3 105.2 %shard_map.95 = (bf16[1,2048,256]{2,1,0:T(8,128)(2,1)}, bf16[512,256]{1,0:T(8,128)(2,1)}, bf16[2048,512]{1,0:T(8,128)(2,1)}, f32[2048,256]{1,0:T(8,128)}) custom-call(f32[16]{0:T(128)} %edge.1, f32[1]{0:T(128)S(6)} %copy.10.step, bf16[1,16,2048]{2,1,0:T(8,128)(2,1)} %tokens.1, bf16[1,16,2048]{2,1,0:T(8,128)(2,1)} %targets.1, bf16[1,2048,256]{2,1,0:T(8,128)(2,1)} %params.1, ...), custom_call_target="tpu_custom_call" | custom-call | tf_op jit(solution)/shard_map/pallas_call | solution.py:609
  106.5 3.8 %shard_map.96 = (bf16[1,2048,256]{2,1,0:T(8,128)(2,1)}, bf16[1,2048,256]{2,1,0:T(8,128)(2,1)}) custom-call(bf16[512,256]{1,0:T(8,128)(2,1)} %get-tuple-element.6.dd_in, bf16[2048,512]{1,0:T(8,128)(2,1)} %get-tuple-element.7.turned_in, f32[2048,256]{1,0:T(8,128)} %get-tuple-element.8.mixed_in, bf16[1,2048,256]{2,1,0:T(8,128)(2,1)} %get-tuple-element.9.fresh_in), custom_call_target="tpu_custom_call" | custom-call | tf_op jit(solution)/shard_map/pallas_call | solution.py:647

commit v4 on v3

--- a/solution.py
+++ b/solution.py
@@ -43,7 +43,7 @@
 DZ, DB, D0 = plan.take(1), plan.take(2), plan.take(2)
 DY, EY = plan.take(2, 4), plan.take(2, 4)
 DX, DF, DC = plan.take(2, 8), plan.take(8), plan.take(8)
-PI, PO, TI, TO, PR = plan.take(1), plan.take(3), plan.take(1), plan.take(1), plan.take(2)
+PI, PO, TI, TO, PR = plan.take(1), plan.take(4), plan.take(1), plan.take(1), plan.take(3)
 HI, BK = plan.take(2), plan.take(2)
 RS, EG = plan.take(2, 3), plan.take(2, 3)
 SEMS = plan.count
@@ -79,6 +79,12 @@
 
     def cols(first, n):
         return pl.ds(first, n)
+
+    barrier = pltpu.get_barrier_semaphore()
+    peers = [other_core, off_chip, other_z, corner, along_x(1), along_x(-1)]
+    peers += [along_y(r) for r in range(1, 8)] + [along_z(1), along_z(-1)]
+    for peer in peers:
+        pl.semaphore_signal(barrier, inc=1, device_id=peer, device_id_type=MESH)
 
     def fetch(src, dst, k):
         copy = pltpu.make_async_copy(src, dst, lsem.at[k])
@@ -98,11 +104,6 @@
                 src = targets.at[0, :, pl.ds(pl.multiple_of(who * 128, 128), 128)]
                 fetch(src, tgt.at[:, cols(rc * 1024 + rx * 256 + rz * 128, 128)], 5)
 
-    barrier = pltpu.get_barrier_semaphore()
-    peers = [other_core, off_chip, other_z, corner, along_x(1), along_x(-1)]
-    peers += [along_y(r) for r in range(1, 8)] + [along_z(1), along_z(-1)]
-    for peer in peers:
-        pl.semaphore_signal(barrier, inc=1, device_id=peer, device_id_type=MESH)
     pl.semaphore_wait(barrier, len(peers))
 
     sent = [0]
@@ -246,22 +247,22 @@
     got_up.wait()
     send(up_own, up_own, other_z, UZ(0))
     got_p.wait()
-    low, quarters = cols(0, 1024), (cols(1024, 512), cols(1536, 512))
-
-    def onward_half(k):
+    low, quarters = cols(0, 512), [cols(512 * k, 512) for k in range(1, 4)]
+
+    def onward_part(k):
         return message(pbuf.at[quarters[k]], prel.at[cols(512 * k, 512)], onward, PR(k), ON_SENT)
 
-    def corner_half(k):
+    def corner_part(k):
         return message(prel.at[cols(512 * k, 512)], pof.at[quarters[k]], corner, PO(1 + k), ON_SENT)
 
-    def straight_half(k):
+    def straight_part(k):
         return message(pbuf.at[quarters[k]], pof.at[quarters[k]], off_chip, PO(1 + k), STRAIGHT_SENT)
 
-    direct_half = message(pbuf.at[low], pof.at[low], off_chip, PO(0), BLOCK_SENT)
+    direct_part = message(pbuf.at[low], pof.at[low], off_chip, PO(0), BLOCK_SENT)
 
     @pl.when(diagonal)
     def _():
-        onward_half(0).start()
+        onward_part(0).start()
 
     send(pbuf, pin, other_core, PI(0))
     got_t.wait()
@@ -277,15 +278,19 @@
         tok_step(way, 1, 3)
         tok_step(way, 1, 1)
 
+    @pl.when(diagonal)
+    def _():
+        onward_part(1).start()
+
     arrive(upb.at[x, 1 - zl, c], UZ(0))
     send(upb.at[x, :, c], upb.at[x, :, c], along_x(1), UX(0))
     send(upb.at[x, :, c], upb.at[x, :, c], along_x(-1), UX(1))
 
     @pl.when(jnp.logical_not(diagonal))
     def _():
-        direct_half.start()
-        straight_half(0).start()
-        straight_half(1).start()
+        direct_part.start()
+        for k in range(3):
+            straight_part(k).start()
 
     tok_finish()
     for way in range(2):
@@ -339,9 +344,10 @@
 
     @pl.when(diagonal)
     def _():
-        onward_half(1).start()
-        arrive(prel.at[cols(0, 512)], PR(0))
-        corner_half(0).start()
+        onward_part(2).start()
+        for k in range(2):
+            arrive(prel.at[cols(512 * k, 512)], PR(k))
+            corner_part(k).start()
 
     token(2, 0)
     x_third(0)
@@ -351,7 +357,7 @@
 
     @pl.when(diagonal)
     def _():
-        direct_half.start()
+        direct_part.start()
 
     token(2, 3, 1)
     x_second(7)
@@ -362,8 +368,8 @@
 
     @pl.when(diagonal)
     def _():
-        arrive(prel.at[cols(512, 512)], PR(1))
-        corner_half(1).start()
+        arrive(prel.at[cols(1024, 512)], PR(2))
+        corner_part(2).start()
 
     token(3, 0, 3)
     x_second(6)
@@ -410,12 +416,9 @@
         hall[p, :, 0:256] = hsend[p, 0:64, :]
 
     hidden_of(0, pbuf)
-    track_piece(0)
     x_second(5)
     x_second(3)
     x_second(4)
-    x_third(6)
-    x_third(2)
 
     e_off = edge[(a + c + 15) % 16]
     e_in = edge[(a + 16 - c) % 16]
@@ -423,7 +426,7 @@
     eta = step[0]
     arrive(pin, PI(0))
     arrive(pof.at[low], PO(0))
-    for k in range(2):
+    for k in range(3):
         arrive(pof.at[quarters[k]], PO(1 + k))
 
     @pl.loop(0, 8)
@@ -436,6 +439,9 @@
     fresh_copy = pltpu.make_async_copy(fresh, fresh_out.at[0], lsem.at[6])
     fresh_copy.start()
     hidden_of(1, fresh)
+    track_piece(0)
+    x_third(6)
+    x_third(2)
     far_wait(4)
     x_third(5)
     x_third(3)
@@ -551,16 +557,16 @@
     for g, nbytes in enumerate(sent):
         if nbytes:
             all_sent(nbytes, g)
-    all_sent(3 << 19, BLOCK_SENT)
+    all_sent(5 << 18, BLOCK_SENT)
     all_sent(14 << 15, BACK_SENT)
 
     @pl.when(diagonal)
     def _():
-        all_sent(1 << 20, ON_SENT)
+        all_sent(3 << 19, ON_SENT)
 
     @pl.when(jnp.logical_not(diagonal))
     def _():
-        all_sent(1 << 19, STRAIGHT_SENT)
+        all_sent(3 << 18, STRAIGHT_SENT)
 
     fresh_copy.wait()
     turned_copy.wait()
@@ -633,7 +639,7 @@
             pltpu.VMEM((2, 512, 256), BF16),
             pltpu.VMEM((2, 512, 256), BF16),
             pltpu.VMEM((512, 256), BF16),
-            pltpu.VMEM((1024, 256), BF16),
+            pltpu.VMEM((1536, 256), BF16),
             pltpu.VMEM((2048, 512), BF16),
             pltpu.VMEM((2048, 256), F32),
             pltpu.SemaphoreType.DMA((SENDS + 4,)),

time: 110 us -> 112 us (1.018)
    pallas_call x1, Pallas kernels: 105 us -> 106 us  [on_device(): pl.pallas_call(kernel, out_shape=(out, jax.ShapeDtypeStruct((512, 256), B...]
where the time goes in v4:
time: 112 us
  Pallas kernels  110 us (98%)
  between operations  1.29 us (1%)
    pallas_call x1, Pallas kernels, on_device(): pl.pallas_call(kernel, out_shape=(out, jax.ShapeDtypeStruct((512, 256), B...  106 us
    pallas_call x1, Pallas kernels, on_device(): pl.pallas_call(last_kernel, out_shape=(out, out), in_specs=[hbm] * 4, out...  3.84 us

profile of v4, /device:TPU:1, one launch (start us, length us, event | category | flops | bytes accessed | tf_op | source)
XLA Modules:
  0.0 111.5 jit_solution(7541543328715409600)
XLA Ops:
  1.3 106.4 %shard_map.95 = (bf16[1,2048,256]{2,1,0:T(8,128)(2,1)}, bf16[512,256]{1,0:T(8,128)(2,1)}, bf16[2048,512]{1,0:T(8,128)(2,1)}, f32[2048,256]{1,0:T(8,128)}) custom-call(f32[16]{0:T(128)} %edge.1, f32[1]{0:T(128)S(6)} %copy.10.step, bf16[1,16,2048]{2,1,0:T(8,128)(2,1)} %tokens.1, bf16[1,16,2048]{2,1,0:T(8,128)(2,1)} %targets.1, bf16[1,2048,256]{2,1,0:T(8,128)(2,1)} %params.1, ...), custom_call_target="tpu_custom_call" | custom-call | tf_op jit(solution)/shard_map/pallas_call | solution.py:615
  107.7 3.8 %shard_map.96 = (bf16[1,2048,256]{2,1,0:T(8,128)(2,1)}, bf16[1,2048,256]{2,1,0:T(8,128)(2,1)}) custom-call(bf16[512,256]{1,0:T(8,128)(2,1)} %get-tuple-element.6.dd_in, bf16[2048,512]{1,0:T(8,128)(2,1)} %get-tuple-element.7.turned_in, f32[2048,256]{1,0:T(8,128)} %get-tuple-element.8.mixed_in, bf16[1,2048,256]{2,1,0:T(8,128)(2,1)} %get-tuple-element.9.fresh_in), custom_call_target="tpu_custom_call" | custom-call | tf_op jit(solution)/shard_map/pallas_call | solution.py:653

commit v5 on v4

--- a/solution.py
+++ b/solution.py
@@ -328,13 +328,6 @@
     def _():
         whole_t.start()
 
-    def track_piece(k):
-        rows = cols(1024 * k, 1024)
-
-        @pl.when(diagonal)
-        def _():
-            message(tbuf.at[rows], tof.at[rows], off_chip, TO(0), BLOCK_SENT).start()
-
     below, above, across = (x + 3) % 4, (x + 1) % 4, (x + 2) % 4
     arrive(upb.at[below, :, c], UX(0))
     send(upb.at[below, 0, c], upb.at[below, 0, c], along_x(1), UF(0))
@@ -365,11 +358,6 @@
     down(4)
     token(2, 2)
     far_wait(1)
-
-    @pl.when(diagonal)
-    def _():
-        arrive(prel.at[cols(1024, 512)], PR(2))
-        corner_part(2).start()
 
     token(3, 0, 3)
     x_second(6)
@@ -380,6 +368,12 @@
     far_wait(2)
     x_third(7)
     x_third(1)
+
+    @pl.when(diagonal)
+    def _():
+        arrive(prel.at[cols(1024, 512)], PR(2))
+        corner_part(2).start()
+
     token(4, 0, 3, 1, 2)
     far_wait(3)
 
@@ -439,7 +433,6 @@
     fresh_copy = pltpu.make_async_copy(fresh, fresh_out.at[0], lsem.at[6])
     fresh_copy.start()
     hidden_of(1, fresh)
-    track_piece(0)
     x_third(6)
     x_third(2)
     far_wait(4)
@@ -499,7 +492,11 @@
     err_of(1)
     for p in range(2):
         err_ring[p][1]()
-    track_piece(1)
+
+    @pl.when(diagonal)
+    def _():
+        whole_t.start()
+
 
     def back_block(p, r):
         return lax.dot_general(
@@ -526,18 +523,23 @@
     back_of(0)
     back_of(1)
 
-    arrive(tin, TI(0))
-    arrive(tof, TO(0))
+    def turn():
+        @pl.loop(0, 8)
+        def _(i):
+            rows = rows256(i)
+            turned[rows, :] = tok[:, rows].T
 
     def prepare():
         @pl.loop(0, 8)
         def _(i):
             rows = rows256(i)
-            turned[rows, :] = tok[:, rows].T
             mixed = own * tbuf[rows, :].astype(F32)
             mixed += e_off * tof[rows, :].astype(F32) + e_in * tin[rows, :].astype(F32)
             mixed_y[rows, :] = mixed
 
+    turn()
+    arrive(tin, TI(0))
+    arrive(tof, TO(0))
     prepare()
     turned_copy = pltpu.make_async_copy(turned, turned_out, lsem.at[7])
     mixed_copy = pltpu.make_async_copy(mixed_y, mixed_out, lsem.at[0])

time: 112 us -> 110 us (0.982)
  the two profiles are of different devices: /device:TPU:1 before, /device:TPU:8 now
where the time goes in v5:
time: 110 us; the launch traced here: 109 us
  Pallas kernels  108 us (98%)
  between operations  1.29 us (1%)
    pallas_call x1, Pallas kernels, on_device(): pl.pallas_call(kernel, out_shape=(out, jax.ShapeDtypeStruct((512, 256), B...  104 us
    pallas_call x1, Pallas kernels, on_device(): pl.pallas_call(last_kernel, out_shape=(out, out), in_specs=[hbm] * 4, out...  3.84 us

profile of v5, /device:TPU:8, one launch (start us, length us, event | category | flops | bytes accessed | tf_op | source)
XLA Modules:
  0.0 109.5 jit_solution(4417284578553826457)
XLA Ops:
  1.3 104.4 %shard_map.95 = (bf16[1,2048,256]{2,1,0:T(8,128)(2,1)}, bf16[512,256]{1,0:T(8,128)(2,1)}, bf16[2048,512]{1,0:T(8,128)(2,1)}, f32[2048,256]{1,0:T(8,128)}) custom-call(f32[16]{0:T(128)} %edge.1, f32[1]{0:T(128)S(6)} %copy.10.step, bf16[1,16,2048]{2,1,0:T(8,128)(2,1)} %tokens.1, bf16[1,16,2048]{2,1,0:T(8,128)(2,1)} %targets.1, bf16[1,2048,256]{2,1,0:T(8,128)(2,1)} %params.1, ...), custom_call_target="tpu_custom_call" | custom-call | tf_op jit(solution)/shard_map/pallas_call | solution.py:617
  105.7 3.8 %shard_map.96 = (bf16[1,2048,256]{2,1,0:T(8,128)(2,1)}, bf16[1,2048,256]{2,1,0:T(8,128)(2,1)}) custom-call(bf16[512,256]{1,0:T(8,128)(2,1)} %get-tuple-element.6.dd_in, bf16[2048,512]{1,0:T(8,128)(2,1)} %get-tuple-element.7.turned_in, f32[2048,256]{1,0:T(8,128)} %get-tuple-element.8.mixed_in, bf16[1,2048,256]{2,1,0:T(8,128)(2,1)} %get-tuple-element.9.fresh_in), custom_call_target="tpu_custom_call" | custom-call | tf_op jit(solution)/shard_map/pallas_call | solution.py:655
